TPU v7x, 16 devices: a whole 2x2x2 slice. The times are simulated.
16 devices in a mesh: rep: 1, dp: 16 (over x, y, z, core).
Axes of the slice: x: 2, y: 2, z: 2, core: 2. Of those that a mesh axis runs over, the one named last changes fastest.
Arguments:
- x: bfloat16 [16, 2048, 896], P(('rep', 'dp'))
- dy: bfloat16 [16, 2048, 896], P(('rep', 'dp'))
- w_gate: bfloat16 [2, 896, 2560], P(None, 'dp')
- w_up: bfloat16 [2, 896, 2560], P(None, 'dp')
- w_down: bfloat16 [2, 2560, 896], P(None, 'dp')
Outputs:
- output 1: bfloat16 [16, 2048, 896], P(('rep', 'dp'))
- output 2: bfloat16 [2, 896, 2560], P('rep', 'dp')
- output 3: bfloat16 [2, 896, 2560], P('rep', 'dp')
- output 4: bfloat16 [2, 2560, 896], P('rep', 'dp')
All inputs are finite; a program needn't handle non-finite values.
Results may differ from a plain program's by a relative error of at most 0.018.
Values are sent between devices in bfloat16 or wider.
A program may use at most 2 GiB of HBM per device.

v0:
```python
import jax
import jax.numpy as jnp
from jax import lax

NAMES = ("w_gate", "w_up", "w_down")


def matmul(a, w):
    return jnp.dot(a, w, preferred_element_type=jnp.float32).astype(jnp.bfloat16)


def normed(h):
    wide = h.astype(jnp.float32)
    scale = lax.rsqrt(jnp.mean(wide**2, -1, keepdims=True) + 1e-6)
    return (wide * scale).astype(jnp.bfloat16)


def layer(h, w):
    a = normed(h)
    gate = jnp.dot(a, w["w_gate"], preferred_element_type=jnp.float32)
    up = jnp.dot(a, w["w_up"], preferred_element_type=jnp.float32)
    return h + matmul((jax.nn.silu(gate) * up).astype(jnp.bfloat16), w["w_down"])


def stack(weights, h):
    for number in range(weights["w_gate"].shape[0]):
        h = layer(h, {name: w[number] for name, w in weights.items()})
    return h


def solution(mesh):
    groups = mesh.shape["rep"]

    def step(x, dy, *weights):
        shape = x.shape
        x, dy = (t.reshape(groups, -1, *t.shape[1:]) for t in (x, dy))

        def of_a_group(x, dy):
            _, back = jax.vjp(stack, dict(zip(NAMES, weights, strict=True)), x)
            by_weights, by_x = back(dy)
            return (by_x, *(by_weights[name] for name in NAMES))

        by_x, *by_weights = jax.vmap(of_a_group)(x, dy)
        return (by_x.reshape(shape), *(t.reshape(-1, *t.shape[2:]) for t in by_weights))

    return step
```

profile of v0, /device:TPU:0, one launch (start us, length us, event | category | flops | bytes accessed | tf_op | source)
XLA Modules:
  0.0 1260.0 jit_solution(12326327031165840382)
XLA Ops:
  39.1 100.6 %while.13 = (bf16[1,2048,896]{2,1,0:T(8,128)(2,1)}, bf16[1,160,896]{2,1,0:T(8,128)(2,1)S(1)}, bf16[1,2048,2560]{1,2,0:T(8,128)(2,1)}, bf16[1,160,896]{2,1,0:T(8,...) while((bf16[1,2048,896]{2,1,0:T(8,128)(2,1)}, ...), condition=%wide.windowed_dot_general_cond_ag, body=%wide.windowed_dot_general_body_ag.sunk | while | flops 2349383680 | bytes 20939292 | solution.py:9
  88.0 8.4 collective-permute-start.2
  139.7 13.8 %copy.2 = bf16[1,2048,2560]{2,1,0:T(8,128)(2,1)} copy(bf16[1,2048,2560]{1,2,0:T(8,128)(2,1)} %get-tuple-element.42) | data formatting | bytes 20971520 | tf_op jit(solution)/vmap(transpose(jvp()))/dot_general | solution.py:9
  153.4 18.2 %fusion.204 = f32[2048,2560]{1,0:T(8,128)} fusion(bf16[1,896,2560]{2,1,0:T(8,128)(2,1)} %all-gather.27.cloned.1.call-done, bf16[1,2048,896]{1,2,0:T(8,128)(2,1)} %fusion.187), kind=kOutput, calls=%fused_computation.257 | convolution fusion | flops 9395240960 | bytes 29229056 | tf_op jit(solution)/vmap(jvp())/dot_general | solution.py:20
  171.6 26.0 %fusion.176 = (bf16[1,2048,2560]{2,1,0:T(8,128)(2,1)}, f32[2048,2560]{1,0:T(8,128)}) fusion(f32[2048,2560]{1,0:T(8,128)} %fusion.204, bf16[1,896,2560]{2,1,0:T(8,128)(2,1)} %all-gather.29.cloned.1.call-done, bf16[1,2048,896]{1,2,0:T(8,128)(2,1)} %fusion.187), kind=kOutput, calls=%fused_computation.215 | convolution fusion | flops 9426698240 | bytes 60686336 | tf_op jit(solution)/vmap(jvp())/dot_general | solution.py:21
  197.7 14.5 %copy.6 = bf16[1,2048,2560]{1,2,0:T(8,128)(2,1)} copy(bf16[1,2048,2560]{2,1,0:T(8,128)(2,1)} %get-tuple-element.281) | data formatting | bytes 20971520
  212.2 15.1 %fusion.189 = (f32[2048]{0:T(1024)S(1)}, bf16[1,2048,896]{1,2,0:T(8,128)(2,1)S(1)}) fusion(bf16[1,2048,896]{1,2,0:T(8,128)(2,1)} %copy.1, bf16[1,2560,896]{2,1,0:T(8,128)(2,1)} %all-gather.31.cloned.1.call-done, bf16[1,2048,2560]{2,1,0:T(8,128)(2,1)} %get-tuple-element.281), kind=kOutput, calls=%fused_computation.242 | convolution fusion | flops 9404413952 | bytes 22421504 | tf_op jit(solution)/vmap(jvp())/dot_general | solution.py:9
  232.1 18.3 %fusion.196 = f32[2048,2560]{1,0:T(8,128)} fusion(bf16[1,896,2560]{2,1,0:T(8,128)(2,1)} %all-gather.33.cloned.1.call-done, bf16[1,2048,896]{1,2,0:T(8,128)(2,1)} %fusion.190), kind=kOutput, calls=%fused_computation.249 | convolution fusion | flops 9395240960 | bytes 29229056 | tf_op jit(solution)/vmap(jvp())/dot_general | solution.py:20
  250.3 26.0 %fusion.170 = (bf16[1,2048,2560]{2,1,0:T(8,128)(2,1)}, f32[2048,2560]{1,0:T(8,128)}) fusion(f32[2048,2560]{1,0:T(8,128)} %fusion.196, bf16[1,896,2560]{2,1,0:T(8,128)(2,1)} %all-gather.35.cloned.1.call-done, bf16[1,2048,896]{1,2,0:T(8,128)(2,1)} %fusion.190), kind=kOutput, calls=%fused_computation.205 | convolution fusion | flops 9426698240 | bytes 60686336 | tf_op jit(solution)/vmap(jvp())/dot_general | solution.py:21
  276.4 14.6 %copy.4 = bf16[1,2048,2560]{1,2,0:T(8,128)(2,1)} copy(bf16[1,2048,2560]{2,1,0:T(8,128)(2,1)} %get-tuple-element.289) | data formatting | bytes 20971520
  291.0 129.6 %while.18 = (bf16[1,2048,2560]{1,2,0:T(8,128)(2,1)}, bf16[1,2048,896]{2,1,0:T(8,128)(2,1)}, f32[160,896]{1,0:T(8,128)S(1)}, f32[160,896]{1,0:T(8,128)}, u32[]{:T...) while((bf16[1,2048,2560]{1,2,0:T(8,128)(2,1)}, ...), condition=%wide.windowed_dot_general_cond_rs.4.clone, body=%wide.windowed_dot_general_body_rs.4.clone.sunk | while | flops 2354913280 | bytes 48955984 | solution.py:9
  291.1 9.0 collective-permute-start.20
  307.6 8.0 collective-permute-start.22
  324.9 8.1 collective-permute-start.20
  356.0 8.1 collective-permute-start.20
  371.6 8.0 collective-permute-start.22
  388.9 8.1 collective-permute-start.20
  404.4 8.0 collective-permute-start.22
  420.6 8.1 collective-permute-start.33
  428.7 19.0 %convert_multiply_fusion.3 = (bf16[1,2048,2560]{2,1,0:T(8,128)(2,1)S(1)}, bf16[1,2048,2560]{2,1,0:T(8,128)(2,1)S(1)}) fusion(f32[2048,2560]{1,0:T(8,128)} %fusion.196, bf16[1,2048,2560]{2,1,0:T(8,128)(2,1)} %copy.2, f32[2048,2560]{1,0:T(8,128)} %get-tuple-element.290), kind=kLoop, calls=%fused_computation.193 | loop fusion | flops 78643200 | bytes 73400320 | tf_op jit(solution)/vmap(transpose(jvp()))/mul | solution.py:22
  447.7 15.0 %fusion.168 = bf16[2048,896]{0,1:T(8,128)(2,1)} fusion(bf16[1,2048,2560]{2,1,0:T(8,128)(2,1)S(1)} %get-tuple-element.622, bf16[1,896,2560]{2,1,0:T(8,128)(2,1)} %all-gather.33.cloned.1.call-done), kind=kOutput, calls=%fused_computation.202 | convolution fusion | flops 9395240960 | bytes 18743296 | tf_op jit(solution)/vmap(transpose(jvp()))/dot_general | solution.py:20
  462.7 14.5 %fusion.191 = (f32[2048]{0:T(1024)S(1)}, bf16[2048,896]{0,1:T(8,128)(2,1)}) fusion(bf16[1,2048,896]{1,2,0:T(8,128)(2,1)} %copy-done.27, bf16[2048,896]{0,1:T(8,128)(2,1)} %fusion.168, bf16[1,896,2560]{2,1,0:T(8,128)(2,1)} %all-gather.35.cloned.1.call-done, bf16[1,2048,2560]{2,1,0:T(8,128)(2,1)S(1)} %get-tuple-element.694), kind=kOutput, calls=%fused_computation.244 | convolution fusion | flops 9404413952 | bytes 26091520 | tf_op jit(solution)/vmap(transpose(jvp()))/dot_general | solution.py:21
  491.1 124.0 %while.19 = (bf16[1,2048,896]{2,1,0:T(8,128)(2,1)}, bf16[1,2048,2560]{1,2,0:T(8,128)(2,1)}, f32[896,160]{0,1:T(8,128)S(1)}, f32[896,160]{0,1:T(8,128)}, u32[]{:T...) while((bf16[1,2048,896]{2,1,0:T(8,128)(2,1)}, ...), condition=%wide.windowed_dot_general_cond_rs.5.clone, body=%wide.windowed_dot_general_body_rs.5.clone.sunk | while | flops 2354913280 | bytes 48955984 | solution.py:9
  502.3 12.1 collective-permute-start.26
  550.8 8.1 collective-permute-start.24
  615.1 8.1 collective-permute-start.34
  623.1 127.3 %while.16 = (bf16[1,2048,2560]{2,1,0:T(8,128)(2,1)}, bf16[1,2048,896]{1,2,0:T(8,128)(2,1)}, f32[2560,56]{0,1:T(8,128)S(1)}, f32[2560,56]{0,1:T(8,128)}, u32[]{:T...) while((bf16[1,2048,2560]{2,1,0:T(8,128)(2,1)}, ...), condition=%wide.windowed_dot_general_cond_rs.2.clone, body=%wide.windowed_dot_general_body_rs.2.clone.sunk | while | flops 2351505408 | bytes 105579144 | solution.py:21
  634.5 12.1 collective-permute-start.14
  685.8 8.1 collective-permute-start.12
  701.4 8.0 collective-permute-start.14
  718.7 8.1 collective-permute-start.12
  734.3 8.0 collective-permute-start.14
  754.9 31.3 %convert_multiply_fusion.1 = (bf16[1,2048,2560]{2,1,0:T(8,128)(2,1)}, bf16[1,2048,2560]{2,1,0:T(8,128)(2,1)}) fusion(f32[2048,2560]{1,0:T(8,128)} %fusion.204, f32[2048,2560]{1,0:T(8,128)} %get-tuple-element.282, bf16[1,2560,896]{2,1,0:T(8,128)(2,1)} %all-gather.31.cloned.1.call-done, bf16[1,2048,896]{1,2,0:T(8,128)(2,1)} %fusion.207), kind=kOutput, calls=%fused_computation.191 | convolution fusion | flops 9479127040 | bytes 71172096 | tf_op jit(solution)/vmap(transpose(jvp()))/dot_general | solution.py:9
  786.2 132.6 %while.17 = (bf16[1,2048,2560]{2,1,0:T(8,128)(2,1)}, bf16[1,2048,896]{1,2,0:T(8,128)(2,1)}, f32[2560,56]{0,1:T(8,128)S(1)}, f32[2560,56]{0,1:T(8,128)}, u32[]{:T...) while((bf16[1,2048,2560]{2,1,0:T(8,128)(2,1)}, ...), condition=%wide.windowed_dot_general_cond_rs.3.clone, body=%wide.windowed_dot_general_body_rs.3.clone.sunk | while | flops 2351505408 | bytes 105579144 | solution.py:21
  797.4 13.1 %collective-permute-start.18 = (f32[2560,56]{0,1:T(8,128)S(1)}, f32[2560,56]{0,1:T(8,128)S(1)}, u32[]{:S(2)}, u32[]{:S(2)}) collective-permute-start(f32[2560,56]{0,1:T(8,128)S(1)} %get-tuple-element.534), channel_id=39, source_target_pairs={{0,1},{1,2},{2,3},{3,4},{4,5},{5,6},{6,7},{7,8},{8,9},{9,10},{10,1... | collective-permute-start | bytes 1720328 | tf_op jit(solution)/vmap(transpose(jvp()))/dot_general | solution.py:21
  831.1 13.7 %collective-permute-start.18 = (f32[2560,56]{0,1:T(8,128)S(1)}, f32[2560,56]{0,1:T(8,128)S(1)}, u32[]{:S(2)}, u32[]{:S(2)}) collective-permute-start(f32[2560,56]{0,1:T(8,128)S(1)} %get-tuple-element.534), channel_id=39, source_target_pairs={{0,1},{1,2},{2,3},{3,4},{4,5},{5,6},{6,7},{7,8},{8,9},{9,10},{10,1... | collective-permute-start | bytes 1720328 | tf_op jit(solution)/vmap(transpose(jvp()))/dot_general | solution.py:21
  865.4 12.1 collective-permute-start.18
  898.2 12.3 collective-permute-start.18
  919.6 128.8 %while.14 = (bf16[1,2048,2560]{2,1,0:T(8,128)(2,1)}, bf16[1,2048,896]{1,2,0:T(8,128)(2,1)}, f32[2560,56]{0,1:T(8,128)S(1)}, f32[2560,56]{0,1:T(8,128)}, u32[]{:T...) while((bf16[1,2048,2560]{2,1,0:T(8,128)(2,1)}, ...), condition=%wide.windowed_dot_general_cond_rs.clone, body=%wide.windowed_dot_general_body_rs.clone.sunk | while | flops 2351505408 | bytes 105579144 | solution.py:20
  951.8 8.1 collective-permute-start.4
  985.0 8.1 collective-permute-start.4
  1017.6 8.1 collective-permute-start.4
  1048.3 132.3 %while.15 = (bf16[1,2048,2560]{2,1,0:T(8,128)(2,1)}, bf16[1,2048,896]{1,2,0:T(8,128)(2,1)}, f32[2560,56]{0,1:T(8,128)S(1)}, f32[2560,56]{0,1:T(8,128)}, u32[]{:T...) while((bf16[1,2048,2560]{2,1,0:T(8,128)(2,1)}, ...), condition=%wide.windowed_dot_general_cond_rs.1.clone, body=%wide.windowed_dot_general_body_rs.1.clone.sunk | while | flops 2351505408 | bytes 105579144 | solution.py:20
  1049.2 8.1 collective-permute-start.8
  1145.2 14.0 %collective-permute-start.8 = (f32[2560,56]{0,1:T(8,128)}, f32[2560,56]{0,1:T(8,128)}, u32[]{:S(2)}, u32[]{:S(2)}) collective-permute-start(f32[2560,56]{0,1:T(8,128)} %broadcast_select_fusion.26), channel_id=25, source_target_pairs={{0,1},{1,2},{2,3},{3,4},{4,5},{5,6},{6,7},{7,8},{8,9},{9,10},{10,1... | collective-permute-start | bytes 1720328 | tf_op jit(solution)/vmap(transpose(jvp()))/dot_general | solution.py:20
  1180.6 12.2 collective-permute-start.32
  1192.8 15.1 %fusion.164 = bf16[2048,896]{0,1:T(8,128)(2,1)} fusion(bf16[1,2048,2560]{2,1,0:T(8,128)(2,1)} %get-tuple-element.810, bf16[1,896,2560]{2,1,0:T(8,128)(2,1)} %all-gather.27.cloned.1.call-done), kind=kOutput, calls=%fused_computation.198 | convolution fusion | flops 9395240960 | bytes 18743296 | tf_op jit(solution)/vmap(transpose(jvp()))/dot_general | solution.py:20
  1208.0 14.3 %fusion.188 = (f32[2048]{0:T(1024)S(1)}, bf16[2048,896]{0,1:T(8,128)(2,1)}) fusion(bf16[1,2048,896]{1,2,0:T(8,128)(2,1)S(1)} %copy-done.11, bf16[2048,896]{0,1:T(8,128)(2,1)} %fusion.164, bf16[1,896,2560]{2,1,0:T(8,128)(2,1)} %all-gather.29.cloned.1.call-done, bf16[1,2048,2560]{2,1,0:T(8,128)(2,1)S(1)} %bitcast.586), kind=kOutput, calls=%fused_computation.241 | convolution fusion | flops 9404413952 | bytes 26091520 | tf_op jit(solution)/vmap(transpose(jvp()))/dot_general | solution.py:21
  (561 shorter events, 731.9 us)
Async XLA Ops:
  7.2 146.3 %all-gather.27.cloned.1.call-start = ((), (), s32[]{:S(2)}) async-start(), calls=%async_computation | async-start | bytes 4874240 | tf_op jit(solution)/vmap(jvp())/squeeze | solution.py:27
  9.1 162.5 %all-gather.29.cloned.1.call-start = ((), (), s32[]{:S(2)}) async-start(), calls=%async_computation.1 | async-start | bytes 4874240 | tf_op jit(solution)/vmap(jvp())/squeeze | solution.py:27
  11.1 201.1 %all-gather.31.cloned.1.call-start = ((), (), s32[]{:S(2)}) async-start(), calls=%async_computation.2 | async-start | bytes 4874240 | tf_op jit(solution)/vmap(jvp())/squeeze | solution.py:27
  13.0 219.1 %all-gather.33.cloned.1.call-start = ((), (), s32[]{:S(2)}) async-start(), calls=%async_computation.3 | async-start | bytes 4874240 | tf_op jit(solution)/vmap(jvp())/squeeze | solution.py:27
  13.6 236.8 %all-gather.35.cloned.1.call-start = ((), (), s32[]{:S(2)}) async-start(), calls=%async_computation.4 | async-start | bytes 4874240 | tf_op jit(solution)/vmap(jvp())/squeeze | solution.py:27
  13.6 20.2 %collective-permute-start.28 = (bf16[1,160,896]{2,1,0:T(8,128)(2,1)S(1)}, bf16[1,160,896]{2,1,0:T(8,128)(2,1)S(1)}, u32[]{:S(2)}, u32[]{:S(2)}) collective-permute-start(bf16[1,160,896]{2,1,0:T(8,128)(2,1)S(1)} %get-tuple-element.557), channel_id=6, source_target_pairs={{0,1},{1,2},{2,3},{3,4},{4,5},{5,6},{6,7},{7,8},{8,9},{9,10},{10,1... | collective-permute-start | bytes 860168 | tf_op jit(solution)/vmap(transpose(jvp()))/dot_general | solution.py:9
  88.0 13.9 %collective-permute-start = (bf16[1,160,896]{2,1,0:T(8,128)(2,1)S(1)}, bf16[1,160,896]{2,1,0:T(8,128)(2,1)S(1)}, u32[]{:S(2)}, u32[]{:S(2)}) collective-permute-start(bf16[1,160,896]{2,1,0:T(8,128)(2,1)S(1)} %get-tuple-element.567), channel_id=7, source_target_pairs={{0,15},{1,0},{2,1},{3,2},{4,3},{5,4},{6,5},{7,6},{8,7},{9,8},{10,9... | collective-permute-start | bytes 860168 | tf_op jit(solution)/vmap(transpose(jvp()))/dot_general | solution.py:9
  88.0 13.9 %collective-permute-start.2 = (bf16[1,160,896]{2,1,0:T(8,128)(2,1)S(1)}, bf16[1,160,896]{2,1,0:T(8,128)(2,1)S(1)}, u32[]{:S(2)}, u32[]{:S(2)}) collective-permute-start(bf16[1,160,896]{2,1,0:T(8,128)(2,1)S(1)} %get-tuple-element.569), channel_id=8, source_target_pairs={{0,1},{1,2},{2,3},{3,4},{4,5},{5,6},{6,7},{7,8},{8,9},{9,10},{10,1... | collective-permute-start | bytes 860168 | tf_op jit(solution)/vmap(transpose(jvp()))/dot_general | solution.py:9
  115.3 12.0 collective-permute-start
  115.3 12.0 collective-permute-start.2
  291.1 13.1 %collective-permute-start.20 = (f32[160,896]{1,0:T(8,128)S(1)}, f32[160,896]{1,0:T(8,128)S(1)}, u32[]{:S(2)}, u32[]{:S(2)}) collective-permute-start(f32[160,896]{1,0:T(8,128)S(1)} %broadcast_select_fusion.32), channel_id=43, source_target_pairs={{0,1},{1,2},{2,3},{3,4},{4,5},{5,6},{6,7},{7,8},{8,9},{9,10},{10,1... | collective-permute-start | bytes 1720328 | tf_op jit(solution)/vmap(transpose(jvp()))/dot_general | solution.py:9
  307.6 12.0 collective-permute-start.22
  324.9 12.2 collective-permute-start.20
  340.4 11.2 collective-permute-start.22
  356.0 12.2 collective-permute-start.20
  371.6 12.0 collective-permute-start.22
  388.9 12.2 collective-permute-start.20
  404.4 12.0 collective-permute-start.22
  420.6 814.5 %collective-permute-start.33 = (f32[160,896]{1,0:T(8,128)}, f32[160,896]{1,0:T(8,128)}, u32[]{:S(2)}, u32[]{:S(2)}) collective-permute-start(f32[160,896]{1,0:T(8,128)} %get-tuple-element.52), channel_id=46, source_target_pairs={{0,1},{1,2},{2,3},{3,4},{4,5},{5,6},{6,7},{7,8},{8,9},{9,10},{10,1... | collective-permute-start | bytes 1720328 | tf_op jit(solution)/vmap(transpose(jvp()))/dot_general | solution.py:9
  502.3 16.1 %collective-permute-start.26 = (f32[896,160]{0,1:T(8,128)S(1)}, f32[896,160]{0,1:T(8,128)S(1)}, u32[]{:S(2)}, u32[]{:S(2)}) collective-permute-start(f32[896,160]{0,1:T(8,128)S(1)} %get-tuple-element.552), channel_id=51, source_target_pairs={{0,1},{1,2},{2,3},{3,4},{4,5},{5,6},{6,7},{7,8},{8,9},{9,10},{10,1... | collective-permute-start | bytes 1720328 | tf_op jit(solution)/vmap(transpose(jvp()))/dot_general | solution.py:9
  523.7 11.2 collective-permute-start.24
  536.7 11.2 collective-permute-start.26
  550.8 16.2 %collective-permute-start.24 = (f32[896,160]{0,1:T(8,128)S(1)}, f32[896,160]{0,1:T(8,128)S(1)}, u32[]{:S(2)}, u32[]{:S(2)}) collective-permute-start(f32[896,160]{0,1:T(8,128)S(1)} %broadcast_select_fusion.34), channel_id=49, source_target_pairs={{0,1},{1,2},{2,3},{3,4},{4,5},{5,6},{6,7},{7,8},{8,9},{9,10},{10,1... | collective-permute-start | bytes 1720328 | tf_op jit(solution)/vmap(transpose(jvp()))/dot_general | solution.py:9
  567.1 15.2 %collective-permute-start.26 = (f32[896,160]{0,1:T(8,128)S(1)}, f32[896,160]{0,1:T(8,128)S(1)}, u32[]{:S(2)}, u32[]{:S(2)}) collective-permute-start(f32[896,160]{0,1:T(8,128)S(1)} %get-tuple-element.552), channel_id=51, source_target_pairs={{0,1},{1,2},{2,3},{3,4},{4,5},{5,6},{6,7},{7,8},{8,9},{9,10},{10,1... | collective-permute-start | bytes 1720328 | tf_op jit(solution)/vmap(transpose(jvp()))/dot_general | solution.py:9
  584.4 11.3 collective-permute-start.24
  599.0 11.9 collective-permute-start.26
  615.1 623.7 %collective-permute-start.34 = (f32[896,160]{0,1:T(8,128)}, f32[896,160]{0,1:T(8,128)}, u32[]{:S(2)}, u32[]{:S(2)}) collective-permute-start(f32[896,160]{0,1:T(8,128)} %get-tuple-element.54), channel_id=52, source_target_pairs={{0,1},{1,2},{2,3},{3,4},{4,5},{5,6},{6,7},{7,8},{8,9},{9,10},{10,1... | collective-permute-start | bytes 1720328 | tf_op jit(solution)/vmap(transpose(jvp()))/dot_general | solution.py:9
  634.5 13.9 %collective-permute-start.14 = (f32[2560,56]{0,1:T(8,128)S(1)}, f32[2560,56]{0,1:T(8,128)S(1)}, u32[]{:S(2)}, u32[]{:S(2)}) collective-permute-start(f32[2560,56]{0,1:T(8,128)S(1)} %get-tuple-element.525), channel_id=33, source_target_pairs={{0,1},{1,2},{2,3},{3,4},{4,5},{5,6},{6,7},{7,8},{8,9},{9,10},{10,1... | collective-permute-start | bytes 1720328 | tf_op jit(solution)/vmap(transpose(jvp()))/dot_general | solution.py:21
  655.9 12.4 collective-permute-start.12
  685.8 14.3 %collective-permute-start.12 = (f32[2560,56]{0,1:T(8,128)S(1)}, f32[2560,56]{0,1:T(8,128)S(1)}, u32[]{:S(2)}, u32[]{:S(2)}) collective-permute-start(f32[2560,56]{0,1:T(8,128)S(1)} %broadcast_select_fusion.28), channel_id=31, source_target_pairs={{0,1},{1,2},{2,3},{3,4},{4,5},{5,6},{6,7},{7,8},{8,9},{9,10},{10,1... | collective-permute-start | bytes 1720328 | tf_op jit(solution)/vmap(transpose(jvp()))/dot_general | solution.py:21
  718.7 14.3 %collective-permute-start.12 = (f32[2560,56]{0,1:T(8,128)S(1)}, f32[2560,56]{0,1:T(8,128)S(1)}, u32[]{:S(2)}, u32[]{:S(2)}) collective-permute-start(f32[2560,56]{0,1:T(8,128)S(1)} %broadcast_select_fusion.28), channel_id=31, source_target_pairs={{0,1},{1,2},{2,3},{3,4},{4,5},{5,6},{6,7},{7,8},{8,9},{9,10},{10,1... | collective-permute-start | bytes 1720328 | tf_op jit(solution)/vmap(transpose(jvp()))/dot_general | solution.py:21
  750.5 486.0 %collective-permute-start.31 = (f32[2560,56]{0,1:T(8,128)}, f32[2560,56]{0,1:T(8,128)}, u32[]{:S(2)}, u32[]{:S(2)}) collective-permute-start(f32[2560,56]{0,1:T(8,128)} %get-tuple-element.48), channel_id=34, source_target_pairs={{0,1},{1,2},{2,3},{3,4},{4,5},{5,6},{6,7},{7,8},{8,9},{9,10},{10,1... | collective-permute-start | bytes 1720328 | tf_op jit(solution)/vmap(transpose(jvp()))/dot_general | solution.py:21
  797.4 14.9 %collective-permute-start.18 = (f32[2560,56]{0,1:T(8,128)S(1)}, f32[2560,56]{0,1:T(8,128)S(1)}, u32[]{:S(2)}, u32[]{:S(2)}) collective-permute-start(f32[2560,56]{0,1:T(8,128)S(1)} %get-tuple-element.534), channel_id=39, source_target_pairs={{0,1},{1,2},{2,3},{3,4},{4,5},{5,6},{6,7},{7,8},{8,9},{9,10},{10,1... | collective-permute-start | bytes 1720328 | tf_op jit(solution)/vmap(transpose(jvp()))/dot_general | solution.py:21
  831.1 15.5 %collective-permute-start.18 = (f32[2560,56]{0,1:T(8,128)S(1)}, f32[2560,56]{0,1:T(8,128)S(1)}, u32[]{:S(2)}, u32[]{:S(2)}) collective-permute-start(f32[2560,56]{0,1:T(8,128)S(1)} %get-tuple-element.534), channel_id=39, source_target_pairs={{0,1},{1,2},{2,3},{3,4},{4,5},{5,6},{6,7},{7,8},{8,9},{9,10},{10,1... | collective-permute-start | bytes 1720328 | tf_op jit(solution)/vmap(transpose(jvp()))/dot_general | solution.py:21
  865.4 13.9 %collective-permute-start.18 = (f32[2560,56]{0,1:T(8,128)S(1)}, f32[2560,56]{0,1:T(8,128)S(1)}, u32[]{:S(2)}, u32[]{:S(2)}) collective-permute-start(f32[2560,56]{0,1:T(8,128)S(1)} %get-tuple-element.534), channel_id=39, source_target_pairs={{0,1},{1,2},{2,3},{3,4},{4,5},{5,6},{6,7},{7,8},{8,9},{9,10},{10,1... | collective-permute-start | bytes 1720328 | tf_op jit(solution)/vmap(transpose(jvp()))/dot_general | solution.py:21
  898.2 14.1 %collective-permute-start.18 = (f32[2560,56]{0,1:T(8,128)S(1)}, f32[2560,56]{0,1:T(8,128)S(1)}, u32[]{:S(2)}, u32[]{:S(2)}) collective-permute-start(f32[2560,56]{0,1:T(8,128)S(1)} %get-tuple-element.534), channel_id=39, source_target_pairs={{0,1},{1,2},{2,3},{3,4},{4,5},{5,6},{6,7},{7,8},{8,9},{9,10},{10,1... | collective-permute-start | bytes 1720328 | tf_op jit(solution)/vmap(transpose(jvp()))/dot_general | solution.py:21
  920.6 12.4 collective-permute-start.4
  951.8 14.9 %collective-permute-start.4 = (f32[2560,56]{0,1:T(8,128)}, f32[2560,56]{0,1:T(8,128)S(1)}, u32[]{:S(2)}, u32[]{:S(2)}) collective-permute-start(f32[2560,56]{0,1:T(8,128)} %broadcast_select_fusion.24), channel_id=19, source_target_pairs={{0,1},{1,2},{2,3},{3,4},{4,5},{5,6},{6,7},{7,8},{8,9},{9,10},{10,1... | collective-permute-start | bytes 1720328 | tf_op jit(solution)/vmap(transpose(jvp()))/dot_general | solution.py:20
  985.0 14.9 %collective-permute-start.4 = (f32[2560,56]{0,1:T(8,128)}, f32[2560,56]{0,1:T(8,128)S(1)}, u32[]{:S(2)}, u32[]{:S(2)}) collective-permute-start(f32[2560,56]{0,1:T(8,128)} %broadcast_select_fusion.24), channel_id=19, source_target_pairs={{0,1},{1,2},{2,3},{3,4},{4,5},{5,6},{6,7},{7,8},{8,9},{9,10},{10,1... | collective-permute-start | bytes 1720328 | tf_op jit(solution)/vmap(transpose(jvp()))/dot_general | solution.py:20
  1017.6 14.9 %collective-permute-start.4 = (f32[2560,56]{0,1:T(8,128)}, f32[2560,56]{0,1:T(8,128)S(1)}, u32[]{:S(2)}, u32[]{:S(2)}) collective-permute-start(f32[2560,56]{0,1:T(8,128)} %broadcast_select_fusion.24), channel_id=19, source_target_pairs={{0,1},{1,2},{2,3},{3,4},{4,5},{5,6},{6,7},{7,8},{8,9},{9,10},{10,1... | collective-permute-start | bytes 1720328 | tf_op jit(solution)/vmap(transpose(jvp()))/dot_general | solution.py:20
  1049.2 14.9 %collective-permute-start.8 = (f32[2560,56]{0,1:T(8,128)}, f32[2560,56]{0,1:T(8,128)}, u32[]{:S(2)}, u32[]{:S(2)}) collective-permute-start(f32[2560,56]{0,1:T(8,128)} %broadcast_select_fusion.26), channel_id=25, source_target_pairs={{0,1},{1,2},{2,3},{3,4},{4,5},{5,6},{6,7},{7,8},{8,9},{9,10},{10,1... | collective-permute-start | bytes 1720328 | tf_op jit(solution)/vmap(transpose(jvp()))/dot_general | solution.py:20
  1082.8 12.2 collective-permute-start.8
  1097.5 12.2 collective-permute-start.10
  1112.5 12.8 %collective-permute-start.8 = (f32[2560,56]{0,1:T(8,128)}, f32[2560,56]{0,1:T(8,128)}, u32[]{:S(2)}, u32[]{:S(2)}) collective-permute-start(f32[2560,56]{0,1:T(8,128)} %broadcast_select_fusion.26), channel_id=25, source_target_pairs={{0,1},{1,2},{2,3},{3,4},{4,5},{5,6},{6,7},{7,8},{8,9},{9,10},{10,1... | collective-permute-start | bytes 1720328 | tf_op jit(solution)/vmap(transpose(jvp()))/dot_general | solution.py:20
  1127.9 11.8 collective-permute-start.10
  1145.2 20.9 %collective-permute-start.8 = (f32[2560,56]{0,1:T(8,128)}, f32[2560,56]{0,1:T(8,128)}, u32[]{:S(2)}, u32[]{:S(2)}) collective-permute-start(f32[2560,56]{0,1:T(8,128)} %broadcast_select_fusion.26), channel_id=25, source_target_pairs={{0,1},{1,2},{2,3},{3,4},{4,5},{5,6},{6,7},{7,8},{8,9},{9,10},{10,1... | collective-permute-start | bytes 1720328 | tf_op jit(solution)/vmap(transpose(jvp()))/dot_general | solution.py:20
  1180.6 57.1 %collective-permute-start.32 = (f32[2560,56]{0,1:T(8,128)}, f32[2560,56]{0,1:T(8,128)}, u32[]{:S(2)}, u32[]{:S(2)}) collective-permute-start(f32[2560,56]{0,1:T(8,128)} %get-tuple-element.50), channel_id=40, source_target_pairs={{0,1},{1,2},{2,3},{3,4},{4,5},{5,6},{6,7},{7,8},{8,9},{9,10},{10,1... | collective-permute-start | bytes 1720328 | tf_op jit(solution)/vmap(transpose(jvp()))/dot_general | solution.py:21
  1235.2 16.9 %collective-permute-start.30 = (f32[2560,56]{0,1:T(8,128)}, f32[2560,56]{0,1:T(8,128)S(1)}, u32[]{:S(2)}, u32[]{:S(2)}) collective-permute-start(f32[2560,56]{0,1:T(8,128)} %get-tuple-element.46), channel_id=28, source_target_pairs={{0,1},{1,2},{2,3},{3,4},{4,5},{5,6},{6,7},{7,8},{8,9},{9,10},{10,1... | collective-permute-start | bytes 1720328 | tf_op jit(solution)/vmap(transpose(jvp()))/dot_general | solution.py:20
  (139 other events, 1872.0 us)
Sparse Core Ops, SparseCore 0:
  10.2 45.0 all-gather.26
  57.5 47.7 all-gather.28
  107.6 45.0 all-gather.30
  154.7 38.9 all-gather.32
  195.8 36.2 all-gather.34
where the time goes:
time: 1270 us; the launch traced here: 1260 us
  starting transfers between devices  425 us (33%)
  matrix products  410 us (32%)
  waiting for transfers between devices  197 us (16%)
  other arithmetic  114 us (9%)
  local copies, waits for them, and re-layouts  96.8 us (8%)
  between operations  14.5 us (1%)
    dot_general x51, starting transfers between devices, matmul(): jnp.dot(a, w, preferred_element_type=jnp.float32).astype(jnp.bfloat16)  172 us
    dot_general x34, starting transfers between devices, layer(): up = jnp.dot(a, w['w_up'], preferred_element_type=jnp.float32)  144 us
    dot_general x20, matrix products, layer(): up = jnp.dot(a, w['w_up'], preferred_element_type=jnp.float32)  143 us
    dot_general x26, matrix products, matmul(): jnp.dot(a, w, preferred_element_type=jnp.float32).astype(jnp.bfloat16)  138 us
    dot_general x20, matrix products, layer(): gate = jnp.dot(a, w['w_gate'], preferred_element_type=jnp.float32)  128 us
    dot_general x34, starting transfers between devices, layer(): gate = jnp.dot(a, w['w_gate'], preferred_element_type=jnp.float32)  109 us
    dot_general x51, waiting for transfers between devices, matmul(): jnp.dot(a, w, preferred_element_type=jnp.float32).astype(jnp.bfloat16)  76.4 us
    dot_general x34, waiting for transfers between devices, layer(): gate = jnp.dot(a, w['w_gate'], preferred_element_type=jnp.float32)  66.7 us
  transfers between devices with their start and end apart: 124, of which 72 were waited for; matrix products, arithmetic and copies ran while one was open for 45% of the time, Pallas kernels for 0%

commit v1 on v0

v1 whole, which is shorter than its diff:
```python
import jax
import jax.numpy as jnp
from jax import lax
from jax.sharding import PartitionSpec as P

NAMES = ("w_gate", "w_up", "w_down")


def dot(a, b, ca, cb):
    return lax.dot_general(a, b, (((ca,), (cb,)), ((), ())), preferred_element_type=jnp.float32)


def solution(mesh):
    def step(x, dy, w_gate, w_up, w_down):
        bf16, f32 = jnp.bfloat16, jnp.float32
        x, dy = x[0], dy[0]
        layers = w_gate.shape[0]
        full = [
            [lax.all_gather(w[l], "dp", axis=0, tiled=True) for w in (w_gate, w_up, w_down)] for l in range(layers)
        ]

        def normed(h):
            wide = h.astype(f32)
            scale = lax.rsqrt(jnp.mean(wide**2, -1, keepdims=True) + 1e-6)
            return (wide * scale).astype(bf16)

        h, kept = x, []
        for l in range(layers):
            wg, wu, wd = full[l]
            a = normed(h)
            gate = dot(a, wg, 1, 0)
            up = dot(a, wu, 1, 0)
            p = (jax.nn.silu(gate) * up).astype(bf16)
            kept.append((h, a, gate, up, p))
            if l + 1 < layers:
                h = h + dot(p, wd, 1, 0).astype(bf16)

        by_h, grads = dy, []
        for l in reversed(range(layers)):
            wg, wu, wd = full[l]
            h, a, gate, up, p = kept[l]
            by_p = dot(by_h, wd, 1, 1).astype(bf16)
            g_down = dot(p, by_h, 0, 0).astype(bf16)
            wide = by_p.astype(f32)
            sig = jax.nn.sigmoid(gate)
            d_up = (wide * (gate * sig)).astype(bf16)
            d_gate = (wide * up * (sig * (1 + gate * (1 - sig)))).astype(bf16)
            g_gate = dot(a, d_gate, 0, 0).astype(bf16)
            g_up = dot(a, d_up, 0, 0).astype(bf16)
            by_a = dot(d_gate, wg, 1, 1).astype(bf16) + dot(d_up, wu, 1, 1).astype(bf16)
            _, back = jax.vjp(normed, h)
            by_h = by_h + back(by_a)[0]
            grads.append([lax.psum_scatter(g, "dp", scatter_dimension=0, tiled=True) for g in (g_gate, g_up, g_down)])
        grads = grads[::-1]
        outs = [jnp.stack([grads[l][i] for l in range(layers)]) for i in range(3)]
        return (by_h[None], *outs)

    tok = P(("rep", "dp"), None, None)
    w = P(None, "dp", None)
    g = P("rep", "dp", None)
    return jax.shard_map(step, mesh=mesh, in_specs=(tok, tok, w, w, w), out_specs=(tok, g, g, g), check_vma=False)
```

time: 1270 us -> 718 us (0.57)
  starting transfers between devices: 425 us -> 0.49 us
  waiting for transfers between devices: 197 us -> 341 us
  other arithmetic: 114 us -> 16.1 us
  matrix products: 410 us -> 313 us
  local copies, waits for them, and re-layouts: 96.8 us -> 26.4 us
    dot_general x119 -> x0, starting transfers between devices: 425 us -> none  [the longest x51 172 us: matmul(): jnp.dot(a, w, preferred_element_type=jnp.float32).astype(jnp.bfloat16)]
    reduce_scatter x0 -> x6, waiting for transfers between devices: none -> 225 us  [step(): lax.psum_scatter(g, 'dp', scatter_dimension=0, tiled=True)]
    dot_general x119 -> x0, waiting for transfers between devices: 197 us -> none  [the longest x51 76.4 us: matmul(): jnp.dot(a, w, preferred_element_type=jnp.float32).astype(jnp.bfloat16)]
    all_gather x0 -> x6, waiting for transfers between devices: none -> 114 us  [step(): lax.all_gather(w[l], 'dp', axis=0, tiled=True)]
    dot_general x66 -> x17, matrix products: 410 us -> 313 us  [dot(): lax.dot_general(a, b, (((ca,), (cb,)), ((), ())), preferred_element_type=...]
    dot_general x96 -> x0, other arithmetic: 65 us -> none
    unnamed x68 -> x25, local copies, waits for them, and re-layouts: 57.6 us -> 20.7 us
    dot_general x82 -> x0, local copies, waits for them, and re-layouts: 33.5 us -> none  [the longest x18 33.4 us: matmul(): jnp.dot(a, w, preferred_element_type=jnp.float32).astype(jnp.bfloat16)]
  transfers between devices with their start and end apart: 124 -> 12, of which waited for: 72 -> 10; matrix products, arithmetic and copies ran while one was open for 45% -> 38% of each run, Pallas kernels for 0% -> 0%
where the time goes in v1:
time: 718 us; the launch traced here: 712 us
  waiting for transfers between devices  341 us (47%)
  matrix products  313 us (44%)
  local copies, waits for them, and re-layouts  26.4 us (4%)
  other arithmetic  16.1 us (2%)
  between operations  14.8 us (2%)
    dot_general x17, matrix products, dot(): lax.dot_general(a, b, (((ca,), (cb,)), ((), ())), preferred_element_type=...  313 us
    reduce_scatter x6, waiting for transfers between devices, step(): lax.psum_scatter(g, 'dp', scatter_dimension=0, tiled=True)  225 us
    all_gather x6, waiting for transfers between devices, step(): lax.all_gather(w[l], 'dp', axis=0, tiled=True)  114 us
    unnamed x25, local copies, waits for them, and re-layouts  20.7 us
  transfers between devices with their start and end apart: 12, of which 10 were waited for; matrix products, arithmetic and copies ran while one was open for 38% of the time, Pallas kernels for 0%

profile of v1, /device:TPU:0, one launch (start us, length us, event | category | flops | bytes accessed | tf_op | source)
XLA Modules:
  0.0 711.9 jit_solution(5077874354530400001)
XLA Ops:
  7.2 1.9 fusion.63
  9.1 0.0 all-gather.17.cloned.1.call-start
  9.2 1.9 fusion.65
  11.1 0.0 all-gather.19.cloned.1.call-start
  11.2 1.9 fusion.64
  13.2 0.5 all-gather.21.cloned.1.call-update
  13.7 0.5 all-gather.23.cloned.1.call-update
  14.3 0.5 all-gather.13.cloned.1.call-update
  14.9 6.1 copy.10
  21.0 2.8 fusion.13
  23.8 0.6 copy-done.6
  24.4 6.2 copy.9
  30.6 19.4 %all-gather.15.cloned.1.call-done = bf16[1,896,2560]{2,1,0:T(8,128)(2,1)} async-done(((bf16[1,56,2560]{2,1,0:T(8,128)(2,1)}), bf16[1,896,2560]{2,1,0:T(8,128)(2,1)}) %all-gather.15.cloned.1.call-update) | async-done | bytes 4587536 | tf_op jit(solution)/shard_map/all_gather | solution.py:19
  49.9 18.0 %fusion.37 = f32[2048,2560]{1,0:T(8,128)} fusion(bf16[1,896,2560]{2,1,0:T(8,128)(2,1)} %all-gather.15.cloned.1.call-done, bf16[1,2048,896]{1,2,0:T(8,128)(2,1)} %copy.10, f32[2048]{0:T(1024)S(1)} %fusion.60), kind=kOutput, calls=%fused_computation.62 | convolution fusion | flops 9400745984 | bytes 29237248 | tf_op jit(solution)/shard_map/dot_general | solution.py:10
  67.9 20.6 %all-gather.17.cloned.1.call-done = bf16[1,896,2560]{2,1,0:T(8,128)(2,1)} async-done(((bf16[1,56,2560]{2,1,0:T(8,128)(2,1)}), bf16[1,896,2560]{2,1,0:T(8,128)(2,1)}) %all-gather.17.cloned.1.call-update) | async-done | bytes 4587536 | tf_op jit(solution)/shard_map/all_gather | solution.py:19
  88.5 28.3 %multiply_convert_fusion.1 = (bf16[2048,2560]{1,0:T(8,128)(2,1)}, f32[2048,2560]{1,0:T(8,128)}) fusion(f32[2048,2560]{1,0:T(8,128)} %fusion.37, bf16[1,896,2560]{2,1,0:T(8,128)(2,1)} %all-gather.17.cloned.1.call-done, bf16[1,2048,896]{1,2,0:T(8,128)(2,1)} %copy.10, f32[2048]{0:T(1024)S(1)} %fusion.60), kind=kOutput, calls=%fused_computation.13 | convolution fusion | flops 9432203264 | bytes 60694528 | tf_op jit(solution)/shard_map/dot_general | solution.py:10
  116.8 10.3 %all-gather.19.cloned.1.call-done = bf16[1,2560,896]{2,1,0:T(8,128)(2,1)} async-done(((bf16[1,160,896]{2,1,0:T(8,128)(2,1)}), bf16[1,2560,896]{2,1,0:T(8,128)(2,1)}) %all-gather.19.cloned.1.call-update) | async-done | bytes 4587536 | tf_op jit(solution)/shard_map/all_gather | solution.py:19
  127.0 16.2 %fusion.16 = (f32[2048]{0:T(1024)S(1)}, bf16[2048,896]{0,1:T(8,128)(2,1)}) fusion(bf16[2048,2560]{1,0:T(8,128)(2,1)} %get-tuple-element.18, bf16[1,2560,896]{2,1,0:T(8,128)(2,1)} %all-gather.19.cloned.1.call-done, bf16[1,2048,896]{1,2,0:T(8,128)(2,1)} %copy.10), kind=kOutput, calls=%fused_computation.36 | convolution fusion | flops 9404413952 | bytes 22421504 | tf_op jit(solution)/shard_map/dot_general | solution.py:10
  143.3 22.8 %all-gather.21.cloned.1.call-done = bf16[1,896,2560]{2,1,0:T(8,128)(2,1)} async-done(((bf16[1,56,2560]{2,1,0:T(8,128)(2,1)}), bf16[1,896,2560]{2,1,0:T(8,128)(2,1)}) %all-gather.21.cloned.1.call-update) | async-done | bytes 4587536 | tf_op jit(solution)/shard_map/all_gather | solution.py:19
  166.0 18.2 %fusion.26 = f32[2048,2560]{1,0:T(8,128)} fusion(bf16[1,896,2560]{2,1,0:T(8,128)(2,1)} %all-gather.21.cloned.1.call-done, bf16[2048,896]{0,1:T(8,128)(2,1)} %get-tuple-element.21, f32[2048]{0:T(1024)S(1)} %fusion.61), kind=kOutput, calls=%fused_computation.51 | convolution fusion | flops 9400745984 | bytes 29237248 | tf_op jit(solution)/shard_map/dot_general | solution.py:10
  184.3 20.7 %all-gather.23.cloned.1.call-done = bf16[1,896,2560]{2,1,0:T(8,128)(2,1)} async-done(((bf16[1,56,2560]{2,1,0:T(8,128)(2,1)}), bf16[1,896,2560]{2,1,0:T(8,128)(2,1)}) %all-gather.23.cloned.1.call-update) | async-done | bytes 4587536 | tf_op jit(solution)/shard_map/all_gather | solution.py:19
  205.0 18.0 %fusion.22 = f32[2048,2560]{1,0:T(8,128)} fusion(bf16[1,896,2560]{2,1,0:T(8,128)(2,1)} %all-gather.23.cloned.1.call-done, bf16[2048,896]{0,1:T(8,128)(2,1)} %get-tuple-element.21, f32[2048]{0:T(1024)S(1)} %fusion.61), kind=kOutput, calls=%fused_computation.47 | convolution fusion | flops 9400745984 | bytes 29237248 | tf_op jit(solution)/shard_map/dot_general | solution.py:10
  223.0 20.4 %all-gather.13.cloned.1.call-done = bf16[1,2560,896]{2,1,0:T(8,128)(2,1)} async-done(((bf16[1,160,896]{2,1,0:T(8,128)(2,1)}), bf16[1,2560,896]{2,1,0:T(8,128)(2,1)}) %all-gather.13.cloned.1.call-update) | async-done | bytes 4587536 | tf_op jit(solution)/shard_map/all_gather | solution.py:19
  243.4 31.4 %fusion.2 = (bf16[2048,2560]{1,0:T(8,128)(2,1)}, bf16[2048,2560]{1,0:T(8,128)(2,1)}) fusion(f32[2048,2560]{1,0:T(8,128)} %fusion.22, f32[2048,2560]{1,0:T(8,128)} %fusion.26, bf16[1,2560,896]{2,1,0:T(8,128)(2,1)} %all-gather.13.cloned.1.call-done, bf16[1,2048,896]{2,1,0:T(8,128)(2,1)} %param.6), kind=kOutput, calls=%fused_computation.6 | convolution fusion | flops 9473884160 | bytes 71172096 | tf_op jit(solution)/shard_map/dot_general | solution.py:10
  274.9 12.5 %fusion.20 = bf16[2048,896]{0,1:T(8,128)(2,1)S(1)} fusion(bf16[2048,2560]{1,0:T(8,128)(2,1)} %get-tuple-element.11, bf16[1,896,2560]{2,1,0:T(8,128)(2,1)S(1)} %copy-done.10), kind=kOutput, calls=%fused_computation.45 | convolution fusion | flops 9395240960 | bytes 18743296 | tf_op jit(solution)/shard_map/dot_general | solution.py:10
  287.4 14.7 %fusion.18 = (f32[2048]{0:T(1024)S(1)}, bf16[2048,896]{0,1:T(8,128)(2,1)S(1)}) fusion(bf16[2048,896]{0,1:T(8,128)(2,1)S(1)} %copy-done.5, bf16[2048,896]{0,1:T(8,128)(2,1)S(1)} %fusion.20, bf16[2048,2560]{1,0:T(8,128)(2,1)} %get-tuple-element.10, bf16[1,896,2560]{2,1,0:T(8,128)(2,1)} %all-gather.21.cloned.1.call-done), kind=kOutput, calls=%fused_computation.38 | convolution fusion | flops 9406248960 | bytes 26091520 | tf_op jit(solution)/shard_map/dot_general | solution.py:10
  302.1 3.0 fusion.42
  305.1 1.8 copy-done.3
  306.9 15.3 %convolution_convert_fusion.2 = bf16[2560,896]{1,0:T(8,128)(2,1)} fusion(bf16[2048,2560]{1,0:T(8,128)(2,1)} %get-tuple-element.18, bf16[2048,896]{0,1:T(8,128)(2,1)S(1)} %fusion.42), kind=kOutput, calls=%fused_computation.40 | convolution fusion | flops 9397534720 | bytes 18743296 | tf_op jit(solution)/shard_map/dot_general | solution.py:10
  322.2 0.0 reduce-scatter.17.cloned.1.call-start
  322.3 21.6 %fusion.19 = bf16[2560,896]{1,0:T(8,128)(2,1)} fusion(f32[2048,2560]{1,0:T(8,128)} %fusion.26, bf16[1,2048,896]{2,1,0:T(8,128)(2,1)} %param.6, f32[2048,2560]{1,0:T(8,128)} %fusion.22), kind=kOutput, calls=%fused_computation.39 | convolution fusion | flops 9428992000 | bytes 50200576 | tf_op jit(solution)/shard_map/dot_general | solution.py:10
  343.9 15.0 %convolution_convert_fusion.3 = bf16[896,2560]{1,0:T(8,128)(2,1)} fusion(bf16[2048,2560]{1,0:T(8,128)(2,1)} %get-tuple-element.10, bf16[2048,896]{0,1:T(8,128)(2,1)} %get-tuple-element.21, f32[2048]{0:T(1024)S(1)} %fusion.61), kind=kOutput, calls=%fused_computation.41 | convolution fusion | flops 9403039744 | bytes 18751488 | tf_op jit(solution)/shard_map/dot_general | solution.py:10
  359.0 31.6 %fusion.4 = (bf16[2048,2560]{1,0:T(8,128)(2,1)}, bf16[2048,2560]{1,0:T(8,128)(2,1)}) fusion(f32[2048,2560]{1,0:T(8,128)} %get-tuple-element.19, f32[2048,2560]{1,0:T(8,128)} %fusion.37, bf16[2048,896]{0,1:T(8,128)(2,1)} %copy-done.3, bf16[1,2560,896]{2,1,0:T(8,128)(2,1)} %all-gather.19.cloned.1.call-done), kind=kOutput, calls=%fused_computation.8 | convolution fusion | flops 9473884160 | bytes 71172096 | tf_op jit(solution)/shard_map/dot_general | solution.py:10
  390.6 13.9 %convolution_convert_fusion.4 = bf16[896,2560]{1,0:T(8,128)(2,1)} fusion(bf16[2048,2560]{1,0:T(8,128)(2,1)} %get-tuple-element.9, bf16[1,2048,896]{1,2,0:T(8,128)(2,1)S(1)} %copy-done, f32[2048]{0:T(1024)S(1)} %copy-done.9), kind=kOutput, calls=%fused_computation.42 | convolution fusion | flops 9403039744 | bytes 18751488 | tf_op jit(solution)/shard_map/dot_general | solution.py:10
  404.4 0.0 reduce-scatter.9.cloned.1.call-start
  404.5 14.9 %convolution_convert_fusion.5 = bf16[896,2560]{1,0:T(8,128)(2,1)} fusion(bf16[2048,2560]{1,0:T(8,128)(2,1)} %get-tuple-element.11, bf16[2048,896]{0,1:T(8,128)(2,1)} %get-tuple-element.21, f32[2048]{0:T(1024)S(1)} %fusion.61), kind=kOutput, calls=%fused_computation.43 | convolution fusion | flops 9403039744 | bytes 18751488 | tf_op jit(solution)/shard_map/dot_general | solution.py:10
  419.5 15.2 %convolution_convert_fusion.6 = bf16[896,2560]{1,0:T(8,128)(2,1)} fusion(bf16[2048,2560]{1,0:T(8,128)(2,1)} %get-tuple-element.8, bf16[1,2048,896]{1,2,0:T(8,128)(2,1)} %copy.10, f32[2048]{0:T(1024)S(1)} %copy-done.9), kind=kOutput, calls=%fused_computation.44 | convolution fusion | flops 9403039744 | bytes 18751488 | tf_op jit(solution)/shard_map/dot_general | solution.py:10
  434.7 13.9 %fusion.31 = bf16[2048,896]{0,1:T(8,128)(2,1)S(1)} fusion(bf16[2048,2560]{1,0:T(8,128)(2,1)} %get-tuple-element.9, bf16[1,896,2560]{2,1,0:T(8,128)(2,1)} %all-gather.17.cloned.1.call-done), kind=kOutput, calls=%fused_computation.56 | convolution fusion | flops 9395240960 | bytes 18743296 | tf_op jit(solution)/shard_map/dot_general | solution.py:10
  448.6 14.3 %fusion.15 = (f32[2048]{0:T(1024)S(1)}, bf16[2048,896]{0,1:T(8,128)(2,1)S(1)}) fusion(bf16[1,2048,896]{1,2,0:T(8,128)(2,1)S(1)} %copy-done.1, bf16[2048,896]{0,1:T(8,128)(2,1)S(1)} %fusion.31, bf16[2048,2560]{1,0:T(8,128)(2,1)} %get-tuple-element.8, bf16[1,896,2560]{2,1,0:T(8,128)(2,1)} %all-gather.15.cloned.1.call-done), kind=kOutput, calls=%fused_computation.35 | convolution fusion | flops 9406248960 | bytes 26091520 | tf_op jit(solution)/shard_map/dot_general | solution.py:10
  462.9 4.6 fusion.41
  467.5 6.0 copy.11
  473.5 1.9 pad_maximum_fusion.2
  475.4 35.8 %reduce-scatter.13.cloned.1.call-done = bf16[56,2560]{1,0:T(8,128)(2,1)} async-done(((bf16[896,2560]{1,0:T(8,128)(2,1)}), bf16[56,2560]{1,0:T(8,128)(2,1)}) %reduce-scatter.13.cloned.1.call-update) | async-done | bytes 286736 | tf_op jit(solution)/shard_map/reduce_scatter | solution.py:53
  511.3 64.1 %reduce-scatter.11.cloned.1.call-done = bf16[56,2560]{1,0:T(8,128)(2,1)} async-done(((bf16[896,2560]{1,0:T(8,128)(2,1)}), bf16[56,2560]{1,0:T(8,128)(2,1)}) %reduce-scatter.11.cloned.1.call-update) | async-done | bytes 286736 | tf_op jit(solution)/shard_map/reduce_scatter | solution.py:53
  575.4 1.9 pad_maximum_fusion.1
  577.3 61.9 %reduce-scatter.9.cloned.1.call-done = bf16[56,2560]{1,0:T(8,128)(2,1)} async-done(((bf16[896,2560]{1,0:T(8,128)(2,1)}), bf16[56,2560]{1,0:T(8,128)(2,1)}) %reduce-scatter.9.cloned.1.call-update) | async-done | bytes 286736 | tf_op jit(solution)/shard_map/reduce_scatter | solution.py:53
  639.2 63.5 %reduce-scatter.7.cloned.1.call-done = bf16[56,2560]{1,0:T(8,128)(2,1)} async-done(((bf16[896,2560]{1,0:T(8,128)(2,1)}), bf16[56,2560]{1,0:T(8,128)(2,1)}) %reduce-scatter.7.cloned.1.call-update) | async-done | bytes 286736 | tf_op jit(solution)/shard_map/reduce_scatter | solution.py:53
  702.7 1.9 pad_maximum_fusion
  (43 shorter events, 0.6 us)
Async XLA Ops:
  7.2 42.8 %all-gather.15.cloned.1.call-start = ((), (), s32[]{:S(2)}) async-start(), calls=%async_computation.13 | async-start | bytes 4874240 | tf_op jit(solution)/shard_map/all_gather | solution.py:19
  9.1 79.4 %all-gather.17.cloned.1.call-start = ((), (), s32[]{:S(2)}) async-start(), calls=%async_computation.14 | async-start | bytes 4874240 | tf_op jit(solution)/shard_map/all_gather | solution.py:19
  11.1 115.9 %all-gather.19.cloned.1.call-start = ((), (), s32[]{:S(2)}) async-start(), calls=%async_computation.15 | async-start | bytes 4874240 | tf_op jit(solution)/shard_map/all_gather | solution.py:19
  13.1 152.9 %all-gather.21.cloned.1.call-start = ((), (), s32[]{:S(2)}) async-start(), calls=%async_computation.16 | async-start | bytes 4874240 | tf_op jit(solution)/shard_map/all_gather | solution.py:19
  13.7 191.3 %all-gather.23.cloned.1.call-start = ((), (), s32[]{:S(2)}) async-start(), calls=%async_computation.17 | async-start | bytes 4874240 | tf_op jit(solution)/shard_map/all_gather | solution.py:19
  14.3 229.1 %all-gather.13.cloned.1.call-start = ((), (), s32[]{:S(2)}) async-start(), calls=%async_computation.12 | async-start | bytes 4874240 | tf_op jit(solution)/shard_map/all_gather | solution.py:19
  14.9 458.7 %reduce-scatter.15.cloned.1.call-start = ((), (), s32[]{:S(2)}) async-start(), calls=%async_computation.10 | async-start | bytes 4874240 | tf_op jit(solution)/shard_map/reduce_scatter | solution.py:53
  23.8 0.6 copy-start.6
  24.4 64.1 %copy-start.8 = (f32[2048]{0:T(1024)}, f32[2048]{0:T(1024)S(1)}, u32[]{:S(2)}) copy-start(f32[2048]{0:T(1024)S(1)} %fusion.60) | copy-start | bytes 24580
  243.4 31.5 %copy-start.10 = (bf16[1,896,2560]{2,1,0:T(8,128)(2,1)S(1)}, bf16[1,896,2560]{2,1,0:T(8,128)(2,1)}, u32[]{:S(2)}) copy-start(bf16[1,896,2560]{2,1,0:T(8,128)(2,1)} %all-gather.23.cloned.1.call-done) | copy-start | bytes 13762564
  274.9 12.5 %copy-start.5 = (bf16[2048,896]{0,1:T(8,128)(2,1)S(1)}, bf16[2048,896]{0,1:T(8,128)(2,1)}, u32[]{:S(2)}) copy-start(bf16[2048,896]{0,1:T(8,128)(2,1)} %get-tuple-element.21) | copy-start | bytes 11010052
  287.4 14.7 %copy-start.2 = (bf16[1,2048,896]{1,2,0:T(8,128)(2,1)S(1)}, bf16[1,2048,896]{1,2,0:T(8,128)(2,1)}, u32[]{:S(2)}) copy-start(bf16[1,2048,896]{1,2,0:T(8,128)(2,1)} %copy.9) | copy-start | bytes 11010052
  305.1 1.8 copy-start.3
  322.2 151.3 %reduce-scatter.17.cloned.1.call-start = ((), (), s32[]{:S(2)}) async-start(), calls=%async_computation.11 | async-start | bytes 4874240 | tf_op jit(solution)/shard_map/reduce_scatter | solution.py:53
  343.9 167.4 %reduce-scatter.13.cloned.1.call-start = ((), (), s32[]{:S(2)}) async-start(), calls=%async_computation.9 | async-start | bytes 4874240 | tf_op jit(solution)/shard_map/reduce_scatter | solution.py:53
  358.9 216.5 %reduce-scatter.11.cloned.1.call-start = ((), (), s32[]{:S(2)}) async-start(), calls=%async_computation.8 | async-start | bytes 4874240 | tf_op jit(solution)/shard_map/reduce_scatter | solution.py:53
  359.0 31.6 %copy-start = (bf16[1,2048,896]{1,2,0:T(8,128)(2,1)S(1)}, bf16[1,2048,896]{1,2,0:T(8,128)(2,1)}, u32[]{:S(2)}) copy-start(bf16[1,2048,896]{1,2,0:T(8,128)(2,1)} %copy.10) | copy-start | bytes 11010052
  359.0 31.6 %copy-start.9 = (f32[2048]{0:T(1024)S(1)}, f32[2048]{0:T(1024)}, u32[]{:S(2)}) copy-start(f32[2048]{0:T(1024)} %copy-done.8) | copy-start | bytes 24580
  404.4 234.7 %reduce-scatter.9.cloned.1.call-start = ((), (), s32[]{:S(2)}) async-start(), calls=%async_computation.7 | async-start | bytes 4874240 | tf_op jit(solution)/shard_map/reduce_scatter | solution.py:53
  419.4 283.3 %reduce-scatter.7.cloned.1.call-start = ((), (), s32[]{:S(2)}) async-start(), calls=%async_computation.6 | async-start | bytes 4874240 | tf_op jit(solution)/shard_map/reduce_scatter | solution.py:53
  434.6 13.9 %copy-start.1 = (bf16[1,2048,896]{1,2,0:T(8,128)(2,1)S(1)}, bf16[1,2048,896]{1,2,0:T(8,128)(2,1)}, u32[]{:S(2)}) copy-start(bf16[1,2048,896]{1,2,0:T(8,128)(2,1)} %copy.10) | copy-start | bytes 11010052
  448.6 14.3 %copy-start.7 = (f32[2048]{0:T(1024)S(1)}, f32[2048]{0:T(1024)}, u32[]{:S(2)}) copy-start(f32[2048]{0:T(1024)} %copy-done.6) | copy-start | bytes 24580
  448.6 14.3 %copy-start.4 = (bf16[2048,896]{0,1:T(8,128)(2,1)S(1)}, bf16[2048,896]{0,1:T(8,128)(2,1)}, u32[]{:S(2)}) copy-start(bf16[2048,896]{0,1:T(8,128)(2,1)} %copy-done.3) | copy-start | bytes 11010052
Sparse Core Ops, SparseCore 0:
  10.8 39.1 all-gather.14
  52.2 36.2 all-gather.16
  90.7 36.2 all-gather.18
  129.7 36.2 all-gather.20
  168.7 36.2 all-gather.22
  207.1 36.2 all-gather.12
  322.3 61.2 reduce-scatter.14
  385.9 61.4 reduce-scatter.16
  449.8 61.4 reduce-scatter.12
  513.4 61.9 reduce-scatter.10
  577.7 61.4 reduce-scatter.8
  641.3 61.3 reduce-scatter.6

commit v2 on v0

v2 whole, which is shorter than its diff:
```python
import functools

import jax
import jax.numpy as jnp
from jax import lax
from jax.experimental import pallas as pl
from jax.experimental.pallas import tpu as pltpu
from jax.sharding import PartitionSpec as P

bf16, f32 = jnp.bfloat16, jnp.float32
MESH = pl.DeviceIdType.MESH
ANY = pl.BlockSpec(memory_space=pl.ANY)
MIB = 1 << 20
CORE, Z, Y, X = 1, 2, 4, 8
ORDERS = ((X, Y, Z), (Y, Z, X), (Z, X, Y))


def thirds(columns):
    tiles = columns // 128
    cuts = [0, (tiles + 2) // 3, (tiles + 2) // 3 + (tiles + 1) // 3, tiles]
    return [(lo * 128, (hi - lo) * 128) for lo, hi in zip(cuts, cuts[1:])]


def bit(me, axis):
    return lax.rem(me // axis, 2)


def flip(me, axis):
    return me + axis - 2 * axis * bit(me, axis)


def subsets(axes):
    sums = [0]
    for axis in axes:
        sums = sums + [s + axis for s in sums]
    return sums


def clear(me, axes):
    for axis in axes:
        me = me - axis * bit(me, axis)
    return me


def meet(me):
    barrier = pltpu.get_barrier_semaphore()
    for axis in (X, Y, Z, CORE):
        pl.semaphore_signal(barrier, inc=1, device_id={"dp": flip(me, axis)}, device_id_type=MESH)
    pl.semaphore_wait(barrier, 4)


class Sends:
    def __init__(self, send, recv):
        self.send, self.recv, self.used = send, recv, 0

    def start(self, source, target, to):
        n = self.used
        self.used += 1
        copy = pltpu.make_async_remote_copy(
            src_ref=source, dst_ref=target, send_sem=self.send.at[n], recv_sem=self.recv.at[n],
            device_id={"dp": to}, device_id_type=MESH,
        )
        copy.start()
        return copy


GATHER_COPIES = 3 * 7 + 8


def gather_kernel(layer, count, *refs):
    shards, fulls = refs[:count], refs[count : 2 * count]
    held, send, recv, local = refs[2 * count : 3 * count], *refs[3 * count :]
    me = lax.axis_index("dp")
    ins = [pltpu.make_async_copy(s.at[layer], h.at[me], local.at[m, 0]) for m, (s, h) in enumerate(zip(shards, held))]
    for copy in ins:
        copy.start()
    meet(me)
    sends = Sends(send, recv)
    flying = [[] for _ in range(count)]
    for stage in range(4):
        for m in range(count):
            if stage == 0:
                ins[m].wait()
            for copy in flying[m]:
                copy.wait()
            flying[m] = []
            if stage < 3:
                for (at, width), order in zip(thirds(held[m].shape[2]), ORDERS):
                    done, axis = order[:stage], order[stage]
                    for s in subsets(done):
                        block = held[m].at[clear(me, done) + s, :, pl.ds(at, width)]
                        flying[m].append(sends.start(block, block, flip(me, axis)))
            else:
                for s in subsets((X, Y, Z)):
                    block = held[m].at[clear(me, (X, Y, Z)) + s]
                    flying[m].append(sends.start(block, block, flip(me, CORE)))
    outs = []
    for m in range(count):
        for s in range(8):
            n = 2 * s + bit(me, CORE)
            outs.append(pltpu.make_async_copy(held[m].at[n], fulls[m].at[n], local.at[m, 1 + s]))
            outs[-1].start()
    for m in range(count):
        for s in range(8):
            flying[m][s].wait()
        for s in range(8):
            n = 2 * s + 1 - bit(me, CORE)
            outs.append(pltpu.make_async_copy(held[m].at[n], fulls[m].at[n], local.at[m, 9 + s]))
            outs[-1].start()
    for copy in outs:
        copy.wait()


def gather(shards, layer, collective_id):
    count = len(shards)
    shapes = [(16, *s.shape[1:]) for s in shards]
    fulls = pl.pallas_call(
        functools.partial(gather_kernel, layer, count),
        out_shape=[jax.ShapeDtypeStruct(s, bf16) for s in shapes],
        in_specs=[ANY] * count,
        out_specs=[ANY] * count,
        scratch_shapes=[pltpu.VMEM(s, bf16) for s in shapes]
        + [pltpu.SemaphoreType.DMA((count * GATHER_COPIES,))] * 2
        + [pltpu.SemaphoreType.DMA((count, 17))],
        compiler_params=pltpu.CompilerParams(collective_id=collective_id, has_side_effects=True, vmem_limit_bytes=60 * MIB),
        cost_estimate=pl.CostEstimate(flops=10 * 10**9 * count, bytes_accessed=10**7 * count, transcendentals=0),
        name="gather",
    )(*shards)
    return [t.reshape(-1, t.shape[2]) for t in fulls]


def scatter_kernel(count, *refs):
    terms, outs = refs[:count], refs[count : 2 * count]
    rest = refs[2 * count :]
    own, other, total, given, got = (rest[k * count : (k + 1) * count] for k in range(5))
    send, recv, local = rest[5 * count :]
    me = lax.axis_index("dp")
    core = bit(me, CORE)
    here = me // 2
    meet(me)
    sends = Sends(send, recv)
    flying, loads = [], []
    for m in range(count):
        flying.append([sends.start(terms[m].at[2 * j + 1 - core], other[m].at[j], flip(me, CORE)) for j in range(8)])
        loads.append([pltpu.make_async_copy(terms[m].at[2 * j + core], own[m].at[j], local.at[m, j]) for j in range(8)])
        for copy in loads[m]:
            copy.start()
    for stage in range(4):
        for m in range(count):
            for copy in flying[m]:
                copy.wait()
            flying[m] = []
            if stage == 0:
                for copy in loads[m]:
                    copy.wait()

                def add(j, _, m=m):
                    total[m][j] = own[m][j].astype(f32) + other[m][j].astype(f32)
                    return 0

                lax.fori_loop(0, 8, add, 0)
            base = (0, 0, 4, 6)[stage]
            cuts = list(zip(thirds(terms[m].shape[2]), ORDERS))
            if stage > 0:
                for (at, width), order in cuts:
                    left = [a // 2 for a in order[stage:]]
                    cols = pl.ds(at, width)
                    for k, s in enumerate(subsets(left)):
                        block = clear(here, left) + s
                        total[m][block, :, cols] = (
                            total[m][block, :, cols] + got[m][(0, 0, 4, 6)[stage] + k, :, cols].astype(f32)
                        )
            if stage < 3:
                base = (0, 4, 6)[stage]
                for (at, width), order in cuts:
                    axis, left = order[stage] // 2, [a // 2 for a in order[stage + 1 :]]
                    cols = pl.ds(at, width)
                    for k, s in enumerate(subsets(left)):
                        given[m][base + k, :, cols] = total[m][flip(clear(here, left), axis) + s, :, cols].astype(bf16)
                for (at, width), order in cuts:
                    cols = pl.ds(at, width)
                    for k in range((4, 2, 1)[stage]):
                        flying[m].append(
                            sends.start(
                                given[m].at[base + k, :, cols], got[m].at[base + k, :, cols], flip(me, order[stage])
                            )
                        )
            else:
                outs[m][...] = total[m][here].astype(bf16)


def scatter(terms, collective_id):
    count = len(terms)
    terms = [t.reshape(16, -1, t.shape[1]) for t in terms]
    blocks = [t.shape[1:] for t in terms]
    vmem = lambda n, dtype: [pltpu.VMEM((n, *b), dtype) for b in blocks]
    return pl.pallas_call(
        functools.partial(scatter_kernel, count),
        out_shape=[jax.ShapeDtypeStruct(b, bf16) for b in blocks],
        in_specs=[ANY] * count,
        out_specs=[pl.BlockSpec(memory_space=pltpu.VMEM)] * count,
        scratch_shapes=vmem(8, bf16) + vmem(8, bf16) + vmem(8, f32) + vmem(7, bf16) + vmem(7, bf16)
        + [pltpu.SemaphoreType.DMA((count * GATHER_COPIES,))] * 2
        + [pltpu.SemaphoreType.DMA((count, 8))],
        compiler_params=pltpu.CompilerParams(collective_id=collective_id, has_side_effects=True, vmem_limit_bytes=60 * MIB),
        cost_estimate=pl.CostEstimate(flops=10 * 10**9 * count, bytes_accessed=10**7 * count, transcendentals=0),
        name="scatter",
    )(*terms)


def dot(a, b, ca, cb):
    return lax.dot_general(a, b, (((ca,), (cb,)), ((), ())), preferred_element_type=f32)


def call(kernel, grid, ins, outs, args, matmuls, name):
    moved = sum(a.size * a.dtype.itemsize for a in args) + sum(
        functools.reduce(lambda p, q: p * q, s, 1) * jnp.dtype(d).itemsize for s, d, _, _ in outs
    )
    return pl.pallas_call(
        kernel,
        grid=grid,
        in_specs=[pl.BlockSpec(b, i) for b, i in ins],
        out_specs=[pl.BlockSpec(b, i) for _, _, b, i in outs],
        out_shape=[jax.ShapeDtypeStruct(s, d) for s, d, _, _ in outs],
        compiler_params=pltpu.CompilerParams(
            dimension_semantics=("arbitrary",) * len(grid), vmem_limit_bytes=56 * MIB
        ),
        cost_estimate=pl.CostEstimate(flops=matmuls * 2 * 2048 * 896 * 2560, bytes_accessed=moved, transcendentals=0),
        name=name,
    )(*args)


def scale_of(wide):
    return lax.rsqrt(jnp.mean(wide * wide, -1, keepdims=True) + 1e-6)


def normed(h):
    wide = h.astype(f32)
    return (wide * scale_of(wide)).astype(bf16)


def backward_of_product(by_p, gate, up):
    wide = by_p.astype(f32)
    sig = jax.nn.sigmoid(gate)
    swish = gate * sig
    by_up = wide * swish
    by_gate = wide * up * (sig + swish * (1 - sig))
    return by_gate.astype(bf16), by_up.astype(bf16)


def forward_kernel(a, wg, wu, gate, up, p):
    gate[...] = dot(a[...], wg[...], 1, 0)
    up[...] = dot(a[...], wu[...], 1, 0)
    g = gate[...]
    p[...] = (g * jax.nn.sigmoid(g) * up[...]).astype(bf16)


def turn_kernel(a, by_h, wg, wu, wd, p, by_gate, by_up):
    g = dot(a[...], wg[...], 1, 0)
    u = dot(a[...], wu[...], 1, 0)
    by_p = dot(by_h[...], wd[...], 1, 1).astype(bf16)
    p[...] = (g * jax.nn.sigmoid(g) * u).astype(bf16)
    by_gate[...], by_up[...] = backward_of_product(by_p, g, u)


def product_kernel(by_h, wd, gate, up, by_gate, by_up):
    by_p = dot(by_h[...], wd[...], 1, 1).astype(bf16)
    by_gate[...], by_up[...] = backward_of_product(by_p, gate[...], up[...])


def down_kernel(p, wd, x, h, a):
    out = x[...] + dot(p[...], wd[...], 1, 0).astype(bf16)
    h[...] = out
    a[...] = normed(out)


def input_kernel(by_gate, by_up, wg, wu, h, by_h, out):
    by_a = dot(by_gate[...], wg[...], 1, 1).astype(bf16) + dot(by_up[...], wu[...], 1, 1).astype(bf16)
    wide, ct = h[...].astype(f32), by_a.astype(f32)
    scale = scale_of(wide)
    by_mean = jnp.sum(ct * wide, -1, keepdims=True) * (-0.5 * scale * scale * scale)
    by_wide = ct * scale + by_mean * (2.0 / wide.shape[1]) * wide
    out[...] = by_h[...] + by_wide.astype(bf16)


def weight_kernel(left, right, out):
    out[...] = dot(left[...], right[...], 0, 0).astype(bf16)


def solution(mesh):
    def step(x, dy, w_gate, w_up, w_down):
        x, dy = x[0], dy[0]
        t, d = x.shape
        ff = w_gate.shape[2]
        bn, bm, bh = 512, 1024, 512

        def whole(w):
            return lax.all_gather(w, "dp", axis=0, tiled=True)

        rows = lambda width: ((bm, width), lambda j, i: (i, 0))
        cols = ((d, bn), lambda j, i: (0, j))
        down = ((bn, d), lambda j, i: (j, 0))
        tile = ((bm, bn), lambda j, i: (i, j))
        slab = lambda width: ((bh, width), lambda i: (i, 0))
        full = lambda a: (a.shape, lambda i: (0, 0))
        both = (ff // bn, t // bm)

        def weight(left, right, name):
            m, n = left.shape[1], right.shape[1]
            if n > m:
                ins, out = [full(left), ((t, bn), lambda j: (0, j))], ((m, bn), lambda j: (0, j))
            else:
                ins, out = [((t, bn), lambda j: (0, j)), full(right)], ((bn, n), lambda j: (j, 0))
            return call(weight_kernel, (ff // bn,), ins, [((m, n), bf16, *out)], (left, right), 1, name)[0]

        def to_input(by_gate, by_up, wg, wu, h, by_h):
            ins = [slab(ff), slab(ff), full(wg), full(wu), slab(d), slab(d)]
            outs = [((t, d), bf16, *slab(d))]
            return call(input_kernel, (t // bh,), ins, outs, (by_gate, by_up, wg, wu, h, by_h), 2, "to_input")[0]

        wg0, wu0 = gather((w_gate, w_up), 0, 0)
        wd0, wg1, wu1, wd1 = whole(w_down[0]), whole(w_gate[1]), whole(w_up[1]), whole(w_down[1])

        a0 = normed(x)
        gate0, up0, p0 = call(
            forward_kernel, both, [rows(d), cols, cols],
            [((t, ff), f32, *tile), ((t, ff), f32, *tile), ((t, ff), bf16, *tile)], (a0, wg0, wu0), 2, "forward",
        )
        h1, a1 = call(
            down_kernel, (t // bh,), [slab(ff), full(wd0), slab(d)], [((t, d), bf16, *slab(d))] * 2, (p0, wd0, x), 1, "down"
        )
        p1, by_gate1, by_up1 = call(
            turn_kernel, both, [rows(d), rows(d), cols, cols, down], [((t, ff), bf16, *tile)] * 3,
            (a1, dy, wg1, wu1, wd1), 3, "turn",
        )
        terms1 = [weight(a1, by_gate1, "g_gate"), weight(a1, by_up1, "g_up"), weight(p1, dy, "g_down")]
        by_gate1, by_up1, *_ = lax.optimization_barrier((by_gate1, by_up1, *terms1))
        grads1 = [lax.psum_scatter(g, "dp", scatter_dimension=0, tiled=True) for g in terms1]
        by_h1 = to_input(by_gate1, by_up1, wg1, wu1, h1, dy)
        by_gate0, by_up0 = call(
            product_kernel, both, [rows(d), down, tile, tile], [((t, ff), bf16, *tile)] * 2, (by_h1, wd0, gate0, up0), 1,
            "product",
        )
        terms0 = [weight(a0, by_gate0, "g_gate"), weight(a0, by_up0, "g_up"), weight(p0, by_h1, "g_down")]
        grads0 = scatter(terms0, 1)
        by_x = to_input(by_gate0, by_up0, wg0, wu0, x, by_h1)
        return (by_x[None], *(jnp.stack([g0, g1]) for g0, g1 in zip(grads0, grads1)))

    tok = P(("rep", "dp"), None, None)
    w = P(None, "dp", None)
    g = P("rep", "dp", None)
    return jax.shard_map(step, mesh=mesh, in_specs=(tok, tok, w, w, w), out_specs=(tok, g, g, g), check_vma=False)
```

time: 1270 us -> 482 us (0.38)
  starting transfers between devices: 425 us -> 0.47 us
  matrix products: 410 us -> 0 us
  Pallas kernels: 0 us -> 397 us
  waiting for transfers between devices: 197 us -> 53.7 us
  other arithmetic: 114 us -> 11.2 us
  local copies, waits for them, and re-layouts: 96.8 us -> 5.45 us
    dot_general x119 -> x0, starting transfers between devices: 425 us -> none  [the longest x51 172 us: matmul(): jnp.dot(a, w, preferred_element_type=jnp.float32).astype(jnp.bfloat16)]
    dot_general x66 -> x0, matrix products: 410 us -> none  [the longest x20 143 us: layer(): up = jnp.dot(a, w['w_up'], preferred_element_type=jnp.float32)]
    pallas_call x0 -> x14, Pallas kernels: none -> 397 us  [the longest x12 283 us: call(): pl.pallas_call(kernel, grid=grid, in_specs=[pl.BlockSpec(b, i) for b, i i...]
    dot_general x119 -> x0, waiting for transfers between devices: 197 us -> none  [the longest x51 76.4 us: matmul(): jnp.dot(a, w, preferred_element_type=jnp.float32).astype(jnp.bfloat16)]
    dot_general x96 -> x0, other arithmetic: 65 us -> none
    unnamed x68 -> x2, local copies, waits for them, and re-layouts: 57.6 us -> 0.15 us
    all_gather x0 -> x4, waiting for transfers between devices: none -> 53.1 us  [whole(): return lax.all_gather(w, 'dp', axis=0, tiled=True)]
    dot_general x82 -> x0, local copies, waits for them, and re-layouts: 33.5 us -> none  [the longest x18 33.4 us: matmul(): jnp.dot(a, w, preferred_element_type=jnp.float32).astype(jnp.bfloat16)]
  transfers between devices with their start and end apart: 124 -> 7, of which waited for: 72 -> 2; matrix products, arithmetic and copies ran while one was open for 45% -> 3% of each run, Pallas kernels for 0% -> 70%
where the time goes in v2:
time: 482 us
  Pallas kernels  397 us (82%)
  waiting for transfers between devices  53.7 us (11%)
  between operations  14.2 us (3%)
  other arithmetic  11.2 us (2%)
  local copies, waits for them, and re-layouts  5.45 us (1%)
    pallas_call x12, Pallas kernels, call(): pl.pallas_call(kernel, grid=grid, in_specs=[pl.BlockSpec(b, i) for b, i i...  283 us
    pallas_call x1, Pallas kernels, scatter(): pl.pallas_call(functools.partial(scatter_kernel, count), out_shape=[jax.S...  59.5 us
    pallas_call x1, Pallas kernels, gather(): pl.pallas_call(functools.partial(gather_kernel, layer, count), out_shape=...  54.3 us
    all_gather x4, waiting for transfers between devices, whole(): return lax.all_gather(w, 'dp', axis=0, tiled=True)  53.1 us
  transfers between devices with their start and end apart: 7, of which 2 were waited for; matrix products, arithmetic and copies ran while one was open for 3% of the time, Pallas kernels for 70%

profile of v2, /device:TPU:0, one launch (start us, length us, event | category | flops | bytes accessed | tf_op | source)
XLA Modules:
  0.0 481.7 jit_solution(12109068516424857385)
XLA Ops:
  7.2 0.0 all-gather.9.cloned.1.call-start
  7.2 1.9 fusion.2
  9.1 0.0 all-gather.9.cloned.1.call-update
  9.1 0.0 all-gather.11.cloned.1.call-start
  9.2 1.7 slice.13
  10.9 0.0 all-gather.11.cloned.1.call-update
  10.9 0.0 all-gather.13.cloned.1.call-start
  10.9 1.7 slice.14
  12.7 0.0 all-gather.13.cloned.1.call-update
  12.7 0.0 all-gather.15.cloned.1.call-start
  12.7 0.5 all-gather.15.cloned.1.call-update
  13.3 0.0 reduce-scatter.4.cloned.1.call-start
  13.3 0.0 copy-start
  13.3 3.0 fusion
  16.3 0.1 copy-done
  16.5 2.5 fusion.1.a.left
  19.0 54.3 %gather.1 = (bf16[16,56,2560]{2,1,0:T(8,128)(2,1)}, bf16[16,56,2560]{2,1,0:T(8,128)(2,1)}) custom-call(bf16[2,56,2560]{2,1,0:T(8,128)(2,1)} %refs_0_.1, bf16[2,56,2560]{2,1,0:T(8,128)(2,1)} %refs_1_.1), custom_call_target="tpu_custom_call" | custom-call | flops 20000000000 | bytes 20000000 | tf_op jit(solution)/shard_map/gather/pallas_call | solution.py:117
  73.3 36.6 %forward.1 = (f32[2048,2560]{1,0:T(8,128)}, f32[2048,2560]{1,0:T(8,128)}, bf16[2048,2560]{1,0:T(8,128)(2,1)}) custom-call(bf16[2048,896]{1,0:T(8,128)(2,1)} %fusion.1.a.left, bf16[896,2560]{1,0:T(8,128)(2,1)} %bitcast.38, bf16[896,2560]{1,0:T(8,128)(2,1)} %bitcast.40), custom_call_target="tpu_custom_call" | custom-call | flops 18790481920 | bytes 65273856 | tf_op jit(solution)/shard_map/forward/pallas_call | solution.py:219
  109.9 0.0 all-gather.9.cloned.1.call-done
  109.9 17.4 %down.1 = (bf16[2048,896]{1,0:T(8,128)(2,1)}, bf16[2048,896]{1,0:T(8,128)(2,1)}) custom-call(bf16[2048,2560]{1,0:T(8,128)(2,1)} %get-tuple-element.23.p.left, bf16[2560,896]{1,0:T(8,128)(2,1)} %bitcast.22, bf16[2048,896]{1,0:T(8,128)(2,1)} %bitcast.20), custom_call_target="tpu_custom_call" | custom-call | flops 9395240960 | bytes 26083328 | tf_op jit(solution)/shard_map/down/pallas_call | solution.py:219
  127.3 0.0 all-gather.11.cloned.1.call-done
  127.3 14.1 %all-gather.13.cloned.1.call-done = bf16[1,896,2560]{2,1,0:T(8,128)(2,1)} async-done(((bf16[1,56,2560]{2,1,0:T(8,128)(2,1)}), bf16[1,896,2560]{2,1,0:T(8,128)(2,1)}) %all-gather.13.cloned.1.call-update) | async-done | bytes 4587536 | tf_op jit(solution)/shard_map/all_gather | solution.py:298
  141.4 39.0 %all-gather.15.cloned.1.call-done = bf16[1,2560,896]{2,1,0:T(8,128)(2,1)} async-done(((bf16[1,160,896]{2,1,0:T(8,128)(2,1)}), bf16[1,2560,896]{2,1,0:T(8,128)(2,1)}) %all-gather.15.cloned.1.call-update) | async-done | bytes 4587536 | tf_op jit(solution)/shard_map/all_gather | solution.py:298
  180.4 43.0 %turn.1 = (bf16[2048,2560]{1,0:T(8,128)(2,1)}, bf16[2048,2560]{1,0:T(8,128)(2,1)}, bf16[2048,2560]{1,0:T(8,128)(2,1)}) custom-call(bf16[2048,896]{1,0:T(8,128)(2,1)} %get-tuple-element.24.a.left, bf16[2048,896]{1,0:T(8,128)(2,1)} %bitcast.35, bf16[896,2560]{1,0:T(8,128)(2,1)} %bitcast.30, bf16[896,2560]{1,0:T(8,128)(2,1)} %bitcast.32, bf16[2560,896]{1,0:T(8,128)(2,1)} %bitcast.34), custom_call_target="tpu_custom_call" | custom-call | flops 28185722880 | bytes 52559872 | tf_op jit(solution)/shard_map/turn/pallas_call | solution.py:219
  223.4 14.2 %g_gate.2 = bf16[896,2560]{1,0:T(8,128)(2,1)} custom-call(bf16[2048,896]{1,0:T(8,128)(2,1)} %get-tuple-element.24.a.left, bf16[2048,2560]{1,0:T(8,128)(2,1)} %get-tuple-element.28.right.by_gate), custom_call_target="tpu_custom_call" | custom-call | flops 9395240960 | bytes 18743296 | tf_op jit(solution)/shard_map/g_gate/pallas_call | solution.py:219
  237.6 0.0 reduce-scatter.4.cloned.1.call-update
  237.6 0.0 reduce-scatter.6.cloned.1.call-start
  237.7 14.2 %g_up.2 = bf16[896,2560]{1,0:T(8,128)(2,1)} custom-call(bf16[2048,896]{1,0:T(8,128)(2,1)} %get-tuple-element.24.a.left, bf16[2048,2560]{1,0:T(8,128)(2,1)} %get-tuple-element.29.right.by_up), custom_call_target="tpu_custom_call" | custom-call | flops 9395240960 | bytes 18743296 | tf_op jit(solution)/shard_map/g_up/pallas_call | solution.py:219
  251.9 0.0 reduce-scatter.6.cloned.1.call-update
  251.9 0.2 reduce-scatter.8.cloned.1.call-start
  252.1 15.6 %g_down.2 = bf16[2560,896]{1,0:T(8,128)(2,1)} custom-call(bf16[2048,2560]{1,0:T(8,128)(2,1)} %get-tuple-element.27.left, bf16[2048,896]{1,0:T(8,128)(2,1)} %bitcast.36), custom_call_target="tpu_custom_call" | custom-call | flops 9395240960 | bytes 18743296 | tf_op jit(solution)/shard_map/g_down/pallas_call | solution.py:219
  267.7 0.0 reduce-scatter.8.cloned.1.call-update
  267.7 32.2 %to_input.2.by_h.right = bf16[2048,896]{1,0:T(8,128)(2,1)} custom-call(bf16[2048,2560]{1,0:T(8,128)(2,1)} %get-tuple-element.28.right.by_gate, bf16[2048,2560]{1,0:T(8,128)(2,1)} %get-tuple-element.29.right.by_up, bf16[896,2560]{1,0:T(8,128)(2,1)} %bitcast.31, bf16[896,2560]{1,0:T(8,128)(2,1)} %bitcast.33, bf16[2048,896]{1,0:T(8,128)(2,1)} %get-tuple-element.30.h, ...), custom_call_target="tpu_custom_call" | custom-call | flops 18790481920 | bytes 41156608 | tf_op jit(solution)/shard_map/to_input/pallas_call | solution.py:219
  299.9 15.5 %g_down.3 = bf16[2560,896]{1,0:T(8,128)(2,1)} custom-call(bf16[2048,2560]{1,0:T(8,128)(2,1)} %get-tuple-element.23.p.left, bf16[2048,896]{1,0:T(8,128)(2,1)} %to_input.2.by_h.right), custom_call_target="tpu_custom_call" | custom-call | flops 9395240960 | bytes 18743296 | tf_op jit(solution)/shard_map/g_down/pallas_call | solution.py:219
  315.4 33.7 %product.1 = (bf16[2048,2560]{1,0:T(8,128)(2,1)}, bf16[2048,2560]{1,0:T(8,128)(2,1)}) custom-call(bf16[2048,896]{1,0:T(8,128)(2,1)} %to_input.2.by_h.right, bf16[2560,896]{1,0:T(8,128)(2,1)} %bitcast.23, f32[2048,2560]{1,0:T(8,128)} %get-tuple-element.31.gate, f32[2048,2560]{1,0:T(8,128)} %get-tuple-element.32.up), custom_call_target="tpu_custom_call" | custom-call | flops 9395240960 | bytes 71172096 | tf_op jit(solution)/shard_map/product/pallas_call | solution.py:219
  349.1 14.2 %g_up.3 = bf16[896,2560]{1,0:T(8,128)(2,1)} custom-call(bf16[2048,896]{1,0:T(8,128)(2,1)} %fusion.1.a.left, bf16[2048,2560]{1,0:T(8,128)(2,1)} %get-tuple-element.34.by_up.right), custom_call_target="tpu_custom_call" | custom-call | flops 9395240960 | bytes 18743296 | tf_op jit(solution)/shard_map/g_up/pallas_call | solution.py:219
  363.2 14.2 %g_gate.3 = bf16[896,2560]{1,0:T(8,128)(2,1)} custom-call(bf16[2048,896]{1,0:T(8,128)(2,1)} %fusion.1.a.left, bf16[2048,2560]{1,0:T(8,128)(2,1)} %get-tuple-element.33.by_gate.right), custom_call_target="tpu_custom_call" | custom-call | flops 9395240960 | bytes 18743296 | tf_op jit(solution)/shard_map/g_gate/pallas_call | solution.py:219
  377.4 32.1 %to_input.3 = bf16[2048,896]{1,0:T(8,128)(2,1)} custom-call(bf16[2048,2560]{1,0:T(8,128)(2,1)} %get-tuple-element.33.by_gate.right, bf16[2048,2560]{1,0:T(8,128)(2,1)} %get-tuple-element.34.by_up.right, bf16[896,2560]{1,0:T(8,128)(2,1)} %bitcast.39, bf16[896,2560]{1,0:T(8,128)(2,1)} %bitcast.41, bf16[2048,896]{1,0:T(8,128)(2,1)} %bitcast.21, ...), custom_call_target="tpu_custom_call" | custom-call | flops 18790481920 | bytes 41156608 | tf_op jit(solution)/shard_map/to_input/pallas_call | solution.py:219
  409.6 59.5 %scatter.1 = (bf16[56,2560]{1,0:T(8,128)(2,1)}, bf16[56,2560]{1,0:T(8,128)(2,1)}, bf16[160,896]{1,0:T(8,128)(2,1)}) custom-call(bf16[16,56,2560]{2,1,0:T(8,128)(2,1)} %bitcast.44, bf16[16,56,2560]{2,1,0:T(8,128)(2,1)} %bitcast.43, bf16[16,160,896]{2,1,0:T(8,128)(2,1)} %bitcast.42), custom_call_target="tpu_custom_call" | custom-call | flops 30000001024 | bytes 30000000 | tf_op jit(solution)/shard_map/scatter/pallas_call | solution.py:197
  469.0 0.0 reduce-scatter.4.cloned.1.call-done
  469.1 1.9 pad_maximum_fusion
  471.0 0.0 reduce-scatter.6.cloned.1.call-done
  471.0 1.9 pad_maximum_fusion.1
  472.9 0.0 reduce-scatter.8.cloned.1.call-done
  472.9 1.9 pad_maximum_fusion.2
  (1 shorter events, 0.0 us)
Async XLA Ops:
  7.2 102.8 %all-gather.9.cloned.1.call-start = ((), (), s32[]{:S(2)}) async-start(), calls=%async_computation.6 | async-start | bytes 4874240 | tf_op jit(solution)/shard_map/all_gather | solution.py:298
  9.1 118.2 %all-gather.11.cloned.1.call-start = ((), (), s32[]{:S(2)}) async-start(), calls=%async_computation.7 | async-start | bytes 4874240 | tf_op jit(solution)/shard_map/all_gather | solution.py:298
  10.9 130.5 %all-gather.13.cloned.1.call-start = ((), (), s32[]{:S(2)}) async-start(), calls=%async_computation.8 | async-start | bytes 4874240 | tf_op jit(solution)/shard_map/all_gather | solution.py:298
  12.7 167.7 %all-gather.15.cloned.1.call-start = ((), (), s32[]{:S(2)}) async-start(), calls=%async_computation.9 | async-start | bytes 4874240 | tf_op jit(solution)/shard_map/all_gather | solution.py:298
  13.3 455.8 %reduce-scatter.4.cloned.1.call-start = ((), (), s32[]{:S(2)}) async-start(), calls=%async_computation.3 | async-start | bytes 4874240 | tf_op jit(solution)/shard_map/reduce_scatter | solution.py:338
  13.3 3.1 copy-start
  237.6 233.4 %reduce-scatter.6.cloned.1.call-start = ((), (), s32[]{:S(2)}) async-start(), calls=%async_computation.4 | async-start | bytes 4874240 | tf_op jit(solution)/shard_map/reduce_scatter | solution.py:338
  251.9 221.0 %reduce-scatter.8.cloned.1.call-start = ((), (), s32[]{:S(2)}) async-start(), calls=%async_computation.5 | async-start | bytes 4874240 | tf_op jit(solution)/shard_map/reduce_scatter | solution.py:338
Sparse Core Ops, SparseCore 0:
  10.8 52.8 all-gather.8
  66.5 36.2 all-gather.10
  105.1 36.2 all-gather.12
  144.0 36.2 all-gather.14
  237.7 61.2 reduce-scatter.3
  301.2 61.8 reduce-scatter.5
  365.4 65.4 reduce-scatter.7

commit v3 on v0

v3 whole, which is shorter than its diff:
```python
import functools

import jax
import jax.numpy as jnp
from jax import lax
from jax.experimental import pallas as pl
from jax.experimental.pallas import tpu as pltpu
from jax.sharding import PartitionSpec as P

bf16, f32 = jnp.bfloat16, jnp.float32
MESH = pl.DeviceIdType.MESH
ANY = pl.BlockSpec(memory_space=pl.ANY)
MIB = 1 << 20
CORE, Z, Y, X = 1, 2, 4, 8
ORDERS = ((X, Y, Z), (Y, Z, X), (Z, X, Y))


def thirds(columns):
    tiles = columns // 128
    cuts = [0, (tiles + 2) // 3, (tiles + 2) // 3 + (tiles + 1) // 3, tiles]
    return [(lo * 128, (hi - lo) * 128) for lo, hi in zip(cuts, cuts[1:])]


def bit(me, axis):
    return lax.rem(me // axis, 2)


def flip(me, axis):
    return me + axis - 2 * axis * bit(me, axis)


def subsets(axes):
    sums = [0]
    for axis in axes:
        sums = sums + [s + axis for s in sums]
    return sums


def chosen(axes, k):
    return sum(axis * lax.rem(k // 2**i, 2) for i, axis in enumerate(axes))


def clear(me, axes):
    for axis in axes:
        me = me - axis * bit(me, axis)
    return me


def meet(me):
    barrier = pltpu.get_barrier_semaphore()
    for axis in (X, Y, Z, CORE):
        pl.semaphore_signal(barrier, inc=1, device_id={"dp": flip(me, axis)}, device_id_type=MESH)
    pl.semaphore_wait(barrier, 4)


class Gather:
    def __init__(self, shards, layer):
        self.args, self.layer, self.count = list(shards), layer, len(shards)
        shapes = [(16, *s.shape[1:]) for s in shards]
        self.in_specs = [ANY] * self.count
        self.outs = [jax.ShapeDtypeStruct(s, bf16) for s in shapes]
        self.out_specs = [ANY] * self.count
        self.scratch = [pltpu.VMEM(s, bf16) for s in shapes] + [
            pltpu.SemaphoreType.DMA((self.count * COPIES,)),
            pltpu.SemaphoreType.DMA((self.count * COPIES,)),
            pltpu.SemaphoreType.DMA((self.count, 17)),
        ]

    def bind(self, shards, fulls, scratch):
        count = self.count
        held, (send, recv, local) = scratch[:count], scratch[count:]
        me = lax.axis_index("dp")

        def ins(m):
            return pltpu.make_async_copy(shards[m].at[self.layer], held[m].at[me], local.at[m, 0])

        def sends(m, stage):
            n = m * COPIES + (0, 3, 9, 21)[stage]
            found = []
            if stage == 3:
                for k, s in enumerate(subsets((X, Y, Z))):
                    block = held[m].at[clear(me, (X, Y, Z)) + s]
                    found.append(remote(block, block, send.at[n + k], recv.at[n + k], flip(me, CORE)))
                return found
            for (at, width), order in zip(thirds(held[m].shape[2]), ORDERS):
                for s in subsets(order[:stage]):
                    block = held[m].at[clear(me, order[:stage]) + s, :, pl.ds(at, width)]
                    k = n + len(found)
                    found.append(remote(block, block, send.at[k], recv.at[k], flip(me, order[stage])))
            return found

        def outs(m, core, at):
            return [
                pltpu.make_async_copy(held[m].at[2 * s + core], fulls[m].at[2 * s + core], local.at[m, at + s])
                for s in range(8)
            ]

        def phase(stage):
            def run():
                if stage == 0:
                    for m in range(count):
                        ins(m).start()
                    meet(me)
                for m in range(count):
                    if stage == 0:
                        ins(m).wait()
                    else:
                        for copy in sends(m, stage - 1):
                            copy.wait()
                    if stage < 4:
                        for copy in sends(m, stage):
                            copy.start()
                    if stage == 3:
                        for copy in outs(m, bit(me, CORE), 1):
                            copy.start()
                    if stage == 4:
                        for copy in outs(m, 1 - bit(me, CORE), 9):
                            copy.start()
                if stage == 4:
                    for m in range(count):
                        for copy in outs(m, bit(me, CORE), 1) + outs(m, 1 - bit(me, CORE), 9):
                            copy.wait()

            return run

        return [phase(stage) for stage in range(5)]


class Scatter:
    def __init__(self, terms):
        self.args = [t.reshape(16, -1, t.shape[1]) for t in terms]
        self.count = len(terms)
        blocks = [t.shape[1:] for t in self.args]
        self.in_specs = [ANY] * self.count
        self.outs = [jax.ShapeDtypeStruct(b, bf16) for b in blocks]
        self.out_specs = [pl.BlockSpec(b, lambda *_: (0, 0)) for b in blocks]
        vmem = lambda n, dtype: [pltpu.VMEM((n, *b), dtype) for b in blocks]
        self.scratch = vmem(8, bf16) + vmem(8, f32) + vmem(8, bf16) + vmem(7, bf16) + [
            pltpu.SemaphoreType.DMA((self.count * COPIES,)),
            pltpu.SemaphoreType.DMA((self.count * COPIES,)),
            pltpu.SemaphoreType.DMA((self.count, 8)),
        ]

    def bind(self, terms, results, scratch):
        count = self.count
        other, total, given, got = (scratch[k * count : (k + 1) * count] for k in range(4))
        send, recv, local = scratch[4 * count :]
        me = lax.axis_index("dp")
        core, here = bit(me, CORE), me // 2

        def loads(m):
            return [pltpu.make_async_copy(terms[m].at[2 * j + core], given[m].at[j], local.at[m, j]) for j in range(8)]

        def sends(m, stage):
            n = m * COPIES + (0, 8, 20, 26)[stage]
            if stage == 0:
                return [
                    remote(terms[m].at[2 * j + 1 - core], other[m].at[j], send.at[n + j], recv.at[n + j], flip(me, CORE))
                    for j in range(8)
                ]
            base, found = (0, 0, 4, 6)[stage], []
            for (at, width), order in zip(thirds(terms[m].shape[2]), ORDERS):
                for k in range((0, 4, 2, 1)[stage]):
                    part = (base + k, slice(None), pl.ds(at, width))
                    i = n + len(found)
                    found.append(remote(given[m].at[part], got[m].at[part], send.at[i], recv.at[i], flip(me, order[stage - 1])))
            return found

        def phase(stage):
            def run():
                if stage == 0:
                    meet(me)
                    for m in range(count):
                        for copy in sends(m, 0) + loads(m):
                            copy.start()
                    return
                for m in range(count):
                    for copy in sends(m, stage - 1):
                        copy.wait()
                    cuts = list(zip(thirds(terms[m].shape[2]), ORDERS))
                    if stage == 1:
                        for copy in loads(m):
                            copy.wait()

                        def add(j, _, m=m):
                            total[m][j] = given[m][j].astype(f32) + other[m][j].astype(f32)
                            return 0

                        lax.fori_loop(0, 8, add, 0)
                    else:
                        for (at, width), order in cuts:
                            left = [axis // 2 for axis in order[stage - 1 :]]
                            cols = pl.ds(at, width)

                            def take(k, _, m=m, left=left, cols=cols):
                                block = clear(here, left) + chosen(left, k)
                                arrived = got[m][(0, 0, 0, 4, 6)[stage] + k, :, cols].astype(f32)
                                total[m][block, :, cols] = total[m][block, :, cols] + arrived
                                return 0

                            lax.fori_loop(0, 2 ** len(left), take, 0)
                    if stage == 4:
                        results[m][...] = total[m][here].astype(bf16)
                        continue
                    base = (0, 0, 4, 6)[stage]
                    for (at, width), order in cuts:
                        axis, left = order[stage - 1] // 2, [a // 2 for a in order[stage:]]
                        cols = pl.ds(at, width)

                        def give(k, _, m=m, axis=axis, left=left, cols=cols):
                            block = flip(clear(here, left), axis) + chosen(left, k)
                            given[m][base + k, :, cols] = total[m][block, :, cols].astype(bf16)
                            return 0

                        lax.fori_loop(0, 2 ** len(left), give, 0)
                    for copy in sends(m, stage):
                        copy.start()

            return run

        return [phase(stage) for stage in range(5)]


def remote(source, target, send, recv, to):
    return pltpu.make_async_remote_copy(
        src_ref=source, dst_ref=target, send_sem=send, recv_sem=recv, device_id={"dp": to}, device_id_type=MESH
    )


COPIES = 3 * 7 + 8


def dot(a, b, ca, cb):
    return lax.dot_general(a, b, (((ca,), (cb,)), ((), ())), preferred_element_type=f32)


def call(kernel, grid, ins, outs, args, matmuls, name, comm=None, steps=(), collective_id=None):
    args, n_in, n_out = list(args), len(args), len(outs)
    moved = sum(a.size * a.dtype.itemsize for a in args) + sum(
        functools.reduce(lambda p, q: p * q, s, 1) * jnp.dtype(d).itemsize for s, d, _, _ in outs
    )
    in_specs = [
        pl.BlockSpec(b, i, pipeline_mode=pl.Buffered(1)) if tuple(b) == a.shape else pl.BlockSpec(b, i)
        for a, (b, i) in zip(args, ins)
    ]
    out_specs = [pl.BlockSpec(b, i) for _, _, b, i in outs]
    out_shape = [jax.ShapeDtypeStruct(s, d) for s, d, _, _ in outs]
    params = dict(dimension_semantics=("arbitrary",) * len(grid), vmem_limit_bytes=58 * MIB)
    body, scratch = kernel, []
    if comm is not None:
        in_specs, out_specs, out_shape = in_specs + comm.in_specs, out_specs + comm.out_specs, out_shape + comm.outs
        args, scratch = args + comm.args, comm.scratch
        params.update(collective_id=collective_id, has_side_effects=True, vmem_limit_bytes=63 * MIB)

        def body(*refs):
            mine, refs = refs[:n_in], refs[n_in:]
            theirs, refs = refs[: comm.count], refs[comm.count :]
            made, refs = refs[:n_out], refs[n_out:]
            phases = comm.bind(theirs, refs[: comm.count], refs[comm.count :])
            step = pl.program_id(0)
            for axis in range(1, len(grid)):
                step = step * grid[axis] + pl.program_id(axis)
            for at, phase in zip(steps, phases):
                if at >= 0:
                    pl.when(step == at)(phase)
            if n_in:
                kernel(*mine, *made)
            for at, phase in zip(steps, phases):
                if at < 0:
                    pl.when(step == -1 - at)(phase)

    return pl.pallas_call(
        body,
        grid=grid,
        in_specs=in_specs,
        out_specs=out_specs,
        out_shape=out_shape,
        scratch_shapes=scratch,
        compiler_params=pltpu.CompilerParams(**params),
        cost_estimate=pl.CostEstimate(
            flops=max(matmuls, 1) * 2 * 2048 * 896 * 2560, bytes_accessed=max(moved, 10**7), transcendentals=0
        ),
        name=name,
    )(*args)


def scale_of(wide):
    return lax.rsqrt(jnp.mean(wide * wide, -1, keepdims=True) + 1e-6)


def normed(h):
    wide = h.astype(f32)
    return (wide * scale_of(wide)).astype(bf16)


def halves(width):
    return [pl.ds(at, 256) for at in range(0, width, 256)]


def forward_kernel(a, wg, wu, swish, slope, p):
    for cols in halves(p.shape[1]):
        g = dot(a[...], wg[:, cols], 1, 0)
        u = dot(a[...], wu[:, cols], 1, 0)
        sig = jax.nn.sigmoid(g)
        s = g * sig
        swish[:, cols] = s
        slope[:, cols] = (0.5 * u) * (sig + s * (1 - sig))
        p[:, cols] = (s * u).astype(bf16)


def turn_kernel(a, by_h, wg, wu, wd, p, by_gate, by_up):
    for cols in halves(p.shape[1]):
        g = dot(a[...], wg[:, cols], 1, 0)
        u = dot(a[...], wu[:, cols], 1, 0)
        by_p = dot(by_h[...], wd[cols, :], 1, 1).astype(bf16).astype(f32)
        sig = jax.nn.sigmoid(g)
        s = g * sig
        p[:, cols] = (s * u).astype(bf16)
        by_up[:, cols] = (by_p * s).astype(bf16)
        by_gate[:, cols] = (by_p * u * (sig + s * (1 - sig))).astype(bf16)


def product_kernel(by_h, wd, swish, slope, by_gate, by_up):
    for cols in halves(by_up.shape[1]):
        by_p = dot(by_h[...], wd[cols, :], 1, 1).astype(bf16).astype(f32)
        by_up[:, cols] = (by_p * swish[:, cols]).astype(bf16)
        by_gate[:, cols] = (by_p * slope[:, cols] * 2).astype(bf16)


def down_kernel(p, wd, x, h, a):
    out = x[...] + dot(p[...], wd[...], 1, 0).astype(bf16)
    h[...] = out
    a[...] = normed(out)


def input_kernel(by_gate, by_up, wg, wu, h, by_h, out):
    by_a = dot(by_gate[...], wg[...], 1, 1).astype(bf16) + dot(by_up[...], wu[...], 1, 1).astype(bf16)
    wide, ct = h[...].astype(f32), by_a.astype(f32)
    scale = scale_of(wide)
    by_mean = jnp.sum(ct * wide, -1, keepdims=True) * (-0.5 * scale * scale * scale)
    by_wide = ct * scale + by_mean * (2.0 / wide.shape[1]) * wide
    out[...] = by_h[...] + by_wide.astype(bf16)


def weight_kernel(left, right, out):
    out[...] = dot(left[...], right[...], 0, 0).astype(bf16)


def solution(mesh):
    def step(x, dy, w_gate, w_up, w_down):
        x, dy = x[0], dy[0]
        t, d = x.shape
        ff = w_gate.shape[2]
        bn, bm, bh = 512, 1024, 512

        def whole(w):
            return lax.all_gather(w, "dp", axis=0, tiled=True)

        rows = lambda width: ((bm, width), lambda j, i: (i, 0))
        cols = ((d, bn), lambda j, i: (0, j))
        down = ((bn, d), lambda j, i: (j, 0))
        tile = ((bm, bn), lambda j, i: (i, j))
        slab = lambda width: ((bh, width), lambda i: (i, 0))
        full = lambda a: (a.shape, lambda i: (0, 0))
        both = (ff // bn, t // bm)

        def weight(left, right, name):
            m, n = left.shape[1], right.shape[1]
            if n > m:
                ins, out = [full(left), ((t, bn), lambda j: (0, j))], ((m, bn), lambda j: (0, j))
            else:
                ins, out = [((t, bn), lambda j: (0, j)), full(right)], ((bn, n), lambda j: (j, 0))
            return call(weight_kernel, (ff // bn,), ins, [((m, n), bf16, *out)], (left, right), 1, name)[0]

        def to_input(by_gate, by_up, wg, wu, h, by_h, comm, steps, collective_id):
            ins = [slab(ff), slab(ff), full(wg), full(wu), slab(d), slab(d)]
            outs = [((t, d), bf16, *slab(d))]
            args = (by_gate, by_up, wg, wu, h, by_h)
            return call(input_kernel, (t // bh,), ins, outs, args, 2, "to_input", comm, steps, collective_id)

        matrix = lambda t: t.reshape(-1, t.shape[2])
        wg0, wu0 = map(matrix, call(None, (1,), [], [], (), 2, "gather", Gather((w_gate, w_up), 0), (0,) * 5, 0))
        wd0, wd1 = whole(w_down[0]), whole(w_down[1])

        a0 = normed(x)
        swish0, slope0, p0, wg1, wu1 = call(
            forward_kernel, both, [rows(d), cols, cols],
            [((t, ff), f32, *tile), ((t, ff), f32, *tile), ((t, ff), bf16, *tile)], (a0, wg0, wu0), 2, "forward",
            Gather((w_gate, w_up), 1), (0, 1, 3, 7, -10), 1,
        )
        wg1, wu1 = matrix(wg1), matrix(wu1)
        h1, a1 = call(
            down_kernel, (t // bh,), [slab(ff), full(wd0), slab(d)], [((t, d), bf16, *slab(d))] * 2, (p0, wd0, x), 1, "down"
        )
        p1, by_gate1, by_up1 = call(
            turn_kernel, both, [rows(d), rows(d), cols, cols, down], [((t, ff), bf16, *tile)] * 3,
            (a1, dy, wg1, wu1, wd1), 3, "turn",
        )
        g_gate1, g_up1 = weight(a1, by_gate1, "g_gate"), weight(a1, by_up1, "g_up")
        p1, _ = lax.optimization_barrier((p1, g_up1))
        g_down1 = weight(p1, dy, "g_down")
        g_gate1, g_up1 = (lax.psum_scatter(g, "dp", scatter_dimension=0, tiled=True) for g in (g_gate1, g_up1))
        by_h1, g_down1 = to_input(by_gate1, by_up1, wg1, wu1, h1, dy, Scatter((g_down1,)), (0, 1, 2, 3, -4), 2)
        g_down0 = weight(p0, by_h1, "g_down")
        by_gate0, by_up0, g_down0 = call(
            product_kernel, both, [rows(d), down, tile, tile], [((t, ff), bf16, *tile)] * 2, (by_h1, wd0, swish0, slope0), 1,
            "product", Scatter((g_down0,)), (0, 2, 5, 7, -10), 3,
        )
        terms0 = [weight(a0, by_gate0, "g_gate"), weight(a0, by_up0, "g_up")]
        by_x, g_gate0, g_up0 = to_input(by_gate0, by_up0, wg0, wu0, x, by_h1, Scatter(terms0), (0, 1, 3, -4, -4), 4)
        grads0, grads1 = (g_gate0, g_up0, g_down0), (g_gate1, g_up1, g_down1)
        return (by_x[None], *(jnp.stack([g0, g1]) for g0, g1 in zip(grads0, grads1)))

    tok = P(("rep", "dp"), None, None)
    w = P(None, "dp", None)
    g = P("rep", "dp", None)
    return jax.shard_map(step, mesh=mesh, in_specs=(tok, tok, w, w, w), out_specs=(tok, g, g, g), check_vma=False)
```

time: 1270 us -> 444 us (0.35)
  starting transfers between devices: 425 us -> 0.34 us
  Pallas kernels: 0 us -> 413 us
  matrix products: 410 us -> 0 us
  waiting for transfers between devices: 197 us -> 0.77 us
  other arithmetic: 114 us -> 10.2 us
  local copies, waits for them, and re-layouts: 96.8 us -> 6.22 us
    dot_general x119 -> x0, starting transfers between devices: 425 us -> none  [the longest x51 172 us: matmul(): jnp.dot(a, w, preferred_element_type=jnp.float32).astype(jnp.bfloat16)]
    pallas_call x0 -> x13, Pallas kernels: none -> 413 us  [call(): pl.pallas_call(body, grid=grid, in_specs=in_specs, out_specs=out_specs, o...]
    dot_general x66 -> x0, matrix products: 410 us -> none  [the longest x20 143 us: layer(): up = jnp.dot(a, w['w_up'], preferred_element_type=jnp.float32)]
    dot_general x119 -> x0, waiting for transfers between devices: 197 us -> none  [the longest x51 76.4 us: matmul(): jnp.dot(a, w, preferred_element_type=jnp.float32).astype(jnp.bfloat16)]
    dot_general x96 -> x0, other arithmetic: 65 us -> none
    unnamed x68 -> x7, local copies, waits for them, and re-layouts: 57.6 us -> 4.32 us
    dot_general x82 -> x0, local copies, waits for them, and re-layouts: 33.5 us -> none  [the longest x18 33.4 us: matmul(): jnp.dot(a, w, preferred_element_type=jnp.float32).astype(jnp.bfloat16)]
    mul x3 -> x0, other arithmetic: 19.1 us -> none  [the longest x1 19 us: layer(): jax.nn.silu(gate) * up]
  transfers between devices with their start and end apart: 124 -> 4, of which waited for: 72 -> 0; matrix products, arithmetic and copies ran while one was open for 45% -> 2% of each run, Pallas kernels for 0% -> 80%
where the time goes in v3:
time: 444 us
  Pallas kernels  413 us (93%)
  between operations  13.8 us (3%)
  other arithmetic  10.2 us (2%)
  local copies, waits for them, and re-layouts  6.22 us (1%)
    pallas_call x13, Pallas kernels, call(): pl.pallas_call(body, grid=grid, in_specs=in_specs, out_specs=out_specs, o...  413 us
  transfers between devices with their start and end apart: 4, of which 0 were waited for; matrix products, arithmetic and copies ran while one was open for 2% of the time, Pallas kernels for 80%

profile of v3, /device:TPU:0, one launch (start us, length us, event | category | flops | bytes accessed | tf_op | source)
XLA Modules:
  0.0 444.1 jit_solution(15174690986312361935)
XLA Ops:
  7.2 0.0 all-gather.5.cloned.1.call-start
  7.2 1.9 fusion.2
  9.1 0.0 all-gather.5.cloned.1.call-update
  9.1 0.0 all-gather.7.cloned.1.call-start
  9.2 0.7 all-gather.7.cloned.1.call-update
  9.9 0.0 reduce-scatter.3.cloned.1.call-start
  9.9 0.0 copy-start
  9.9 3.0 fusion
  12.9 0.1 copy-done
  13.1 2.5 fusion.1.refs_0_.left
  15.6 55.9 %gather.1 = (bf16[16,56,2560]{2,1,0:T(8,128)(2,1)}, bf16[16,56,2560]{2,1,0:T(8,128)(2,1)}) custom-call(bf16[2,56,2560]{2,1,0:T(8,128)(2,1)} %refs_3_.1, bf16[2,56,2560]{2,1,0:T(8,128)(2,1)} %refs_4_.1), custom_call_target="tpu_custom_call" | custom-call | flops 18790481920 | bytes 10000000 | tf_op jit(solution)/shard_map/gather/pallas_call | solution.py:272
  71.5 62.9 %forward.1 = (f32[2048,2560]{1,0:T(8,128)}, f32[2048,2560]{1,0:T(8,128)}, bf16[2048,2560]{1,0:T(8,128)(2,1)}, bf16[16,56,2560]{2,1,0:T(8,128)(2,1)}, bf16[16,56,2560]{2,1,0:T(8,128)(2,1)}) custom-call(bf16[2048,896]{1,0:T(8,128)(2,1)} %fusion.1.refs_0_.left, bf16[896,2560]{1,0:T(8,128)(2,1)} %bitcast.37, bf16[896,2560]{1,0:T(8,128)(2,1)} %bitcast.39, ...), custom_call_target="tpu_custom_call" | custom-call | flops 18790481920 | bytes 65273856 | tf_op jit(solution)/shard_map/forward/pallas_call | solution.py:272
  134.4 0.0 all-gather.5.cloned.1.call-done
  134.5 17.4 %down.1 = (bf16[2048,896]{1,0:T(8,128)(2,1)}, bf16[2048,896]{1,0:T(8,128)(2,1)}) custom-call(bf16[2048,2560]{1,0:T(8,128)(2,1)} %get-tuple-element.27.p.left, bf16[2560,896]{1,0:T(8,128)(2,1)} %bitcast.23, bf16[2048,896]{1,0:T(8,128)(2,1)} %bitcast.21), custom_call_target="tpu_custom_call" | custom-call | flops 9395240960 | bytes 26083328 | tf_op jit(solution)/shard_map/down/pallas_call | solution.py:272
  151.9 0.0 all-gather.7.cloned.1.call-done
  151.9 42.0 %turn.1 = (bf16[2048,2560]{1,0:T(8,128)(2,1)}, bf16[2048,2560]{1,0:T(8,128)(2,1)}, bf16[2048,2560]{1,0:T(8,128)(2,1)}) custom-call(bf16[2048,896]{1,0:T(8,128)(2,1)} %get-tuple-element.28.a.left, bf16[2048,896]{1,0:T(8,128)(2,1)} %bitcast.34, bf16[896,2560]{1,0:T(8,128)(2,1)} %bitcast.41, bf16[896,2560]{1,0:T(8,128)(2,1)} %bitcast.43, bf16[2560,896]{1,0:T(8,128)(2,1)} %bitcast.33), custom_call_target="tpu_custom_call" | custom-call | flops 28185722880 | bytes 52559872 | tf_op jit(solution)/shard_map/turn/pallas_call | solution.py:272
  193.8 14.2 %g_gate.3 = bf16[896,2560]{1,0:T(8,128)(2,1)} custom-call(bf16[2048,896]{1,0:T(8,128)(2,1)} %get-tuple-element.28.a.left, bf16[2048,2560]{1,0:T(8,128)(2,1)} %get-tuple-element.31.refs_0_.right), custom_call_target="tpu_custom_call" | custom-call | flops 9395240960 | bytes 18743296 | tf_op jit(solution)/shard_map/g_gate/pallas_call | solution.py:272
  208.0 0.0 reduce-scatter.3.cloned.1.call-update
  208.0 0.2 reduce-scatter.5.cloned.1.call-start
  208.3 14.2 %g_up.2 = bf16[896,2560]{1,0:T(8,128)(2,1)} custom-call(bf16[2048,896]{1,0:T(8,128)(2,1)} %get-tuple-element.28.a.left, bf16[2048,2560]{1,0:T(8,128)(2,1)} %get-tuple-element.32.right.refs_1_), custom_call_target="tpu_custom_call" | custom-call | flops 9395240960 | bytes 18743296 | tf_op jit(solution)/shard_map/g_up/pallas_call | solution.py:272
  222.5 0.0 reduce-scatter.5.cloned.1.call-update
  222.5 15.5 %g_down.2 = bf16[2560,896]{1,0:T(8,128)(2,1)} custom-call(bf16[2048,2560]{1,0:T(8,128)(2,1)} %get-tuple-element.35.left, bf16[2048,896]{1,0:T(8,128)(2,1)} %bitcast.35), custom_call_target="tpu_custom_call" | custom-call | flops 9395240960 | bytes 18743296 | tf_op jit(solution)/shard_map/g_down/pallas_call | solution.py:272
  238.0 48.1 %to_input.2 = (bf16[2048,896]{1,0:T(8,128)(2,1)}, bf16[160,896]{1,0:T(8,128)(2,1)}) custom-call(bf16[2048,2560]{1,0:T(8,128)(2,1)} %get-tuple-element.31.refs_0_.right, bf16[2048,2560]{1,0:T(8,128)(2,1)} %get-tuple-element.32.right.refs_1_, bf16[896,2560]{1,0:T(8,128)(2,1)} %bitcast.42, bf16[896,2560]{1,0:T(8,128)(2,1)} %bitcast.44, ...), custom_call_target="tpu_custom_call" | custom-call | flops 18790481920 | bytes 41156608 | tf_op jit(solution)/shard_map/to_input/pallas_call | solution.py:272
  286.1 15.5 %g_down.3 = bf16[2560,896]{1,0:T(8,128)(2,1)} custom-call(bf16[2048,2560]{1,0:T(8,128)(2,1)} %get-tuple-element.27.p.left, bf16[2048,896]{1,0:T(8,128)(2,1)} %get-tuple-element.36.right.refs_0_.refs_5_), custom_call_target="tpu_custom_call" | custom-call | flops 9395240960 | bytes 18743296 | tf_op jit(solution)/shard_map/g_down/pallas_call | solution.py:272
  301.5 48.4 %product.1 = (bf16[2048,2560]{1,0:T(8,128)(2,1)}, bf16[2048,2560]{1,0:T(8,128)(2,1)}, bf16[160,896]{1,0:T(8,128)(2,1)}) custom-call(bf16[2048,896]{1,0:T(8,128)(2,1)} %get-tuple-element.36.right.refs_0_.refs_5_, bf16[2560,896]{1,0:T(8,128)(2,1)} %bitcast.24, f32[2048,2560]{1,0:T(8,128)} %get-tuple-element.37.refs_2_, ...), custom_call_target="tpu_custom_call" | custom-call | flops 9395240960 | bytes 71172096 | tf_op jit(solution)/shard_map/product/pallas_call | solution.py:272
  349.9 14.4 %g_gate.2 = bf16[896,2560]{1,0:T(8,128)(2,1)} custom-call(bf16[2048,896]{1,0:T(8,128)(2,1)} %fusion.1.refs_0_.left, bf16[2048,2560]{1,0:T(8,128)(2,1)} %get-tuple-element.39.right.refs_0_), custom_call_target="tpu_custom_call" | custom-call | flops 9395240960 | bytes 18743296 | tf_op jit(solution)/shard_map/g_gate/pallas_call | solution.py:272
  364.3 14.1 %g_up.3 = bf16[896,2560]{1,0:T(8,128)(2,1)} custom-call(bf16[2048,896]{1,0:T(8,128)(2,1)} %fusion.1.refs_0_.left, bf16[2048,2560]{1,0:T(8,128)(2,1)} %get-tuple-element.40.right.refs_1_), custom_call_target="tpu_custom_call" | custom-call | flops 9395240960 | bytes 18743296 | tf_op jit(solution)/shard_map/g_up/pallas_call | solution.py:272
  378.4 0.0 copy-start.1
  378.4 0.0 copy-start.2
  378.4 50.3 %to_input.3 = (bf16[2048,896]{1,0:T(8,128)(2,1)}, bf16[56,2560]{1,0:T(8,128)(2,1)}, bf16[56,2560]{1,0:T(8,128)(2,1)}) custom-call(bf16[2048,2560]{1,0:T(8,128)(2,1)} %get-tuple-element.39.right.refs_0_, bf16[2048,2560]{1,0:T(8,128)(2,1)} %get-tuple-element.40.right.refs_1_, bf16[896,2560]{1,0:T(8,128)(2,1)} %bitcast.38, bf16[896,2560]{1,0:T(8,128)(2,1)} %bitcast.40, ...), custom_call_target="tpu_custom_call" | custom-call | flops 18790481920 | bytes 41156608 | tf_op jit(solution)/shard_map/to_input/pallas_call | solution.py:272
  428.7 0.0 copy-done.1
  428.7 0.0 copy-done.2
  428.7 0.9 pad_maximum_fusion.2
  429.6 0.0 reduce-scatter.3.cloned.1.call-done
  429.6 1.9 pad_maximum_fusion
  431.5 0.0 reduce-scatter.5.cloned.1.call-done
  431.5 1.9 pad_maximum_fusion.1
  433.4 4.2 copy.10
  (1 shorter events, 0.0 us)
Async XLA Ops:
  7.2 127.3 %all-gather.5.cloned.1.call-start = ((), (), s32[]{:S(2)}) async-start(), calls=%async_computation.4 | async-start | bytes 4874240 | tf_op jit(solution)/shard_map/all_gather | solution.py:357
  9.1 142.7 %all-gather.7.cloned.1.call-start = ((), (), s32[]{:S(2)}) async-start(), calls=%async_computation.5 | async-start | bytes 4874240 | tf_op jit(solution)/shard_map/all_gather | solution.py:357
  9.9 419.7 %reduce-scatter.3.cloned.1.call-start = ((), (), s32[]{:S(2)}) async-start(), calls=%async_computation.2 | async-start | bytes 4874240 | tf_op jit(solution)/shard_map/reduce_scatter | solution.py:402
  9.9 3.1 copy-start
  208.0 223.5 %reduce-scatter.5.cloned.1.call-start = ((), (), s32[]{:S(2)}) async-start(), calls=%async_computation.3 | async-start | bytes 4874240 | tf_op jit(solution)/shard_map/reduce_scatter | solution.py:402
  378.4 50.3 %copy-start.1 = (bf16[160,896]{1,0:T(8,128)(2,1)S(1)}, bf16[160,896]{1,0:T(8,128)(2,1)}, u32[]{:S(2)}) copy-start(bf16[160,896]{1,0:T(8,128)(2,1)} %get-tuple-element.45) | copy-start | bytes 860164
  378.4 50.3 %copy-start.2 = (bf16[160,896]{1,0:T(8,128)(2,1)S(1)}, bf16[160,896]{1,0:T(8,128)(2,1)}, u32[]{:S(2)}) copy-start(bf16[160,896]{1,0:T(8,128)(2,1)} %get-tuple-element.44) | copy-start | bytes 860164
Sparse Core Ops, SparseCore 0:
  10.8 53.9 all-gather.4
  67.6 52.2 all-gather.6
  208.2 66.8 reduce-scatter.2
  277.2 73.2 reduce-scatter.4

commit v4 on v3

--- a/solution.py
+++ b/solution.py
@@ -54,8 +54,8 @@
 
 
 class Gather:
-    def __init__(self, shards, layer):
-        self.args, self.layer, self.count = list(shards), layer, len(shards)
+    def __init__(self, shards, layers):
+        self.args, self.layers, self.count = list(shards), layers, len(shards)
         shapes = [(16, *s.shape[1:]) for s in shards]
         self.in_specs = [ANY] * self.count
         self.outs = [jax.ShapeDtypeStruct(s, bf16) for s in shapes]
@@ -72,7 +72,7 @@
         me = lax.axis_index("dp")
 
         def ins(m):
-            return pltpu.make_async_copy(shards[m].at[self.layer], held[m].at[me], local.at[m, 0])
+            return pltpu.make_async_copy(shards[m].at[self.layers[m]], held[m].at[me], local.at[m, 0])
 
         def sends(m, stage):
             n = m * COPIES + (0, 3, 9, 21)[stage]
@@ -379,16 +379,17 @@
             return call(input_kernel, (t // bh,), ins, outs, args, 2, "to_input", comm, steps, collective_id)
 
         matrix = lambda t: t.reshape(-1, t.shape[2])
-        wg0, wu0 = map(matrix, call(None, (1,), [], [], (), 2, "gather", Gather((w_gate, w_up), 0), (0,) * 5, 0))
-        wd0, wd1 = whole(w_down[0]), whole(w_down[1])
+        wg0, wu0 = map(matrix, call(None, (1,), [], [], (), 2, "gather", Gather((w_gate, w_up), (0, 0)), (0,) * 5, 0))
+        late, wg0 = lax.optimization_barrier((w_down[1], wg0))
+        wd1 = whole(late)
 
         a0 = normed(x)
-        swish0, slope0, p0, wg1, wu1 = call(
+        swish0, slope0, p0, wd0, wg1, wu1 = call(
             forward_kernel, both, [rows(d), cols, cols],
             [((t, ff), f32, *tile), ((t, ff), f32, *tile), ((t, ff), bf16, *tile)], (a0, wg0, wu0), 2, "forward",
-            Gather((w_gate, w_up), 1), (0, 1, 3, 7, -10), 1,
+            Gather((w_down, w_gate, w_up), (0, 1, 1)), (0, 1, 3, 7, -10), 1,
         )
-        wg1, wu1 = matrix(wg1), matrix(wu1)
+        wd0, wg1, wu1 = matrix(wd0), matrix(wg1), matrix(wu1)
         h1, a1 = call(
             down_kernel, (t // bh,), [slab(ff), full(wd0), slab(d)], [((t, d), bf16, *slab(d))] * 2, (p0, wd0, x), 1, "down"
         )

time: 444 us -> 446 us (level)
  transfers between devices with their start and end apart: 4 -> 3, of which waited for: 0 -> 0; matrix products, arithmetic and copies ran while one was open for 2% -> 2% of each run, Pallas kernels for 80% -> 71%
where the time goes in v4:
time: 446 us; the launch traced here: 445 us
  Pallas kernels  415 us (93%)
  between operations  13.8 us (3%)
  other arithmetic  10.2 us (2%)
  local copies, waits for them, and re-layouts  6.02 us (1%)
    pallas_call x13, Pallas kernels, call(): pl.pallas_call(body, grid=grid, in_specs=in_specs, out_specs=out_specs, o...  415 us
  transfers between devices with their start and end apart: 3, of which 0 were waited for; matrix products, arithmetic and copies ran while one was open for 2% of the time, Pallas kernels for 71%

profile of v4, /device:TPU:0, one launch (start us, length us, event | category | flops | bytes accessed | tf_op | source)
XLA Modules:
  0.0 445.4 jit_solution(11671242326647239288)
XLA Ops:
  7.2 0.0 all-gather.2.cloned.1.call-start
  7.2 1.7 slice_bitcast_fusion
  8.9 41.6 %gather.1 = (bf16[16,56,2560]{2,1,0:T(8,128)(2,1)}, bf16[16,56,2560]{2,1,0:T(8,128)(2,1)}) custom-call(bf16[2,56,2560]{2,1,0:T(8,128)(2,1)} %refs_4_.1, bf16[2,56,2560]{2,1,0:T(8,128)(2,1)} %refs_5_.1), custom_call_target="tpu_custom_call" | custom-call | flops 18790481920 | bytes 10000000 | tf_op jit(solution)/shard_map/gather/pallas_call | solution.py:272
  50.5 0.0 all-gather.2.cloned.1.call-update
  50.5 0.0 reduce-scatter.3.cloned.1.call-start
  50.5 0.0 copy-start
  50.6 3.0 fusion
  53.5 0.1 copy-done
  53.7 2.5 fusion.1.refs_0_.left
  56.2 78.2 %forward.1 = (f32[2048,2560]{1,0:T(8,128)}, f32[2048,2560]{1,0:T(8,128)}, bf16[2048,2560]{1,0:T(8,128)(2,1)}, bf16[16,160,896]{2,1,0:T(8,128)(2,1)}, bf16[16,56,...) custom-call(bf16[2048,896]{1,0:T(8,128)(2,1)} %fusion.1.refs_0_.left, bf16[896,2560]{1,0:T(8,128)(2,1)} %bitcast.37, ...), custom_call_target="tpu_custom_call" | custom-call | flops 18790481920 | bytes 65273856 | tf_op jit(solution)/shard_map/forward/pallas_call | solution.py:272
  134.4 17.4 %down.1 = (bf16[2048,896]{1,0:T(8,128)(2,1)}, bf16[2048,896]{1,0:T(8,128)(2,1)}) custom-call(bf16[2048,2560]{1,0:T(8,128)(2,1)} %get-tuple-element.31.p.left, bf16[2560,896]{1,0:T(8,128)(2,1)} %bitcast.24, bf16[2048,896]{1,0:T(8,128)(2,1)} %bitcast.22), custom_call_target="tpu_custom_call" | custom-call | flops 9395240960 | bytes 26083328 | tf_op jit(solution)/shard_map/down/pallas_call | solution.py:272
  151.8 0.0 all-gather.2.cloned.1.call-done.wd
  151.8 42.0 %turn.1 = (bf16[2048,2560]{1,0:T(8,128)(2,1)}, bf16[2048,2560]{1,0:T(8,128)(2,1)}, bf16[2048,2560]{1,0:T(8,128)(2,1)}) custom-call(bf16[2048,896]{1,0:T(8,128)(2,1)} %get-tuple-element.33.a.left, bf16[2048,896]{1,0:T(8,128)(2,1)} %bitcast.34, bf16[896,2560]{1,0:T(8,128)(2,1)} %bitcast.41, bf16[896,2560]{1,0:T(8,128)(2,1)} %bitcast.43, ...), custom_call_target="tpu_custom_call" | custom-call | flops 28185722880 | bytes 52559872 | tf_op jit(solution)/shard_map/turn/pallas_call | solution.py:272
  193.8 14.2 %g_gate.3 = bf16[896,2560]{1,0:T(8,128)(2,1)} custom-call(bf16[2048,896]{1,0:T(8,128)(2,1)} %get-tuple-element.33.a.left, bf16[2048,2560]{1,0:T(8,128)(2,1)} %get-tuple-element.37.refs_0_.right), custom_call_target="tpu_custom_call" | custom-call | flops 9395240960 | bytes 18743296 | tf_op jit(solution)/shard_map/g_gate/pallas_call | solution.py:272
  208.0 0.0 reduce-scatter.3.cloned.1.call-update
  208.0 0.2 reduce-scatter.5.cloned.1.call-start
  208.2 14.2 %g_up.2 = bf16[896,2560]{1,0:T(8,128)(2,1)} custom-call(bf16[2048,896]{1,0:T(8,128)(2,1)} %get-tuple-element.33.a.left, bf16[2048,2560]{1,0:T(8,128)(2,1)} %get-tuple-element.38.right.refs_1_), custom_call_target="tpu_custom_call" | custom-call | flops 9395240960 | bytes 18743296 | tf_op jit(solution)/shard_map/g_up/pallas_call | solution.py:272
  222.4 0.0 reduce-scatter.5.cloned.1.call-update
  222.4 15.5 %g_down.2 = bf16[2560,896]{1,0:T(8,128)(2,1)} custom-call(bf16[2048,2560]{1,0:T(8,128)(2,1)} %get-tuple-element.41.left, bf16[2048,896]{1,0:T(8,128)(2,1)} %bitcast.35), custom_call_target="tpu_custom_call" | custom-call | flops 9395240960 | bytes 18743296 | tf_op jit(solution)/shard_map/g_down/pallas_call | solution.py:272
  237.9 48.1 %to_input.2 = (bf16[2048,896]{1,0:T(8,128)(2,1)}, bf16[160,896]{1,0:T(8,128)(2,1)}) custom-call(bf16[2048,2560]{1,0:T(8,128)(2,1)} %get-tuple-element.37.refs_0_.right, bf16[2048,2560]{1,0:T(8,128)(2,1)} %get-tuple-element.38.right.refs_1_, bf16[896,2560]{1,0:T(8,128)(2,1)} %bitcast.42, bf16[896,2560]{1,0:T(8,128)(2,1)} %bitcast.44, ...), custom_call_target="tpu_custom_call" | custom-call | flops 18790481920 | bytes 41156608 | tf_op jit(solution)/shard_map/to_input/pallas_call | solution.py:272
  286.1 15.5 %g_down.3 = bf16[2560,896]{1,0:T(8,128)(2,1)} custom-call(bf16[2048,2560]{1,0:T(8,128)(2,1)} %get-tuple-element.31.p.left, bf16[2048,896]{1,0:T(8,128)(2,1)} %get-tuple-element.42.right.refs_0_.refs_5_), custom_call_target="tpu_custom_call" | custom-call | flops 9395240960 | bytes 18743296 | tf_op jit(solution)/shard_map/g_down/pallas_call | solution.py:272
  301.5 48.1 %product.1 = (bf16[2048,2560]{1,0:T(8,128)(2,1)}, bf16[2048,2560]{1,0:T(8,128)(2,1)}, bf16[160,896]{1,0:T(8,128)(2,1)}) custom-call(bf16[2048,896]{1,0:T(8,128)(2,1)} %get-tuple-element.42.right.refs_0_.refs_5_, bf16[2560,896]{1,0:T(8,128)(2,1)} %bitcast.25, f32[2048,2560]{1,0:T(8,128)} %get-tuple-element.43.refs_2_, ...), custom_call_target="tpu_custom_call" | custom-call | flops 9395240960 | bytes 71172096 | tf_op jit(solution)/shard_map/product/pallas_call | solution.py:272
  349.7 14.4 %g_gate.2 = bf16[896,2560]{1,0:T(8,128)(2,1)} custom-call(bf16[2048,896]{1,0:T(8,128)(2,1)} %fusion.1.refs_0_.left, bf16[2048,2560]{1,0:T(8,128)(2,1)} %get-tuple-element.45.right.refs_0_), custom_call_target="tpu_custom_call" | custom-call | flops 9395240960 | bytes 18743296 | tf_op jit(solution)/shard_map/g_gate/pallas_call | solution.py:272
  364.1 14.2 %g_up.3 = bf16[896,2560]{1,0:T(8,128)(2,1)} custom-call(bf16[2048,896]{1,0:T(8,128)(2,1)} %fusion.1.refs_0_.left, bf16[2048,2560]{1,0:T(8,128)(2,1)} %get-tuple-element.46.right.refs_1_), custom_call_target="tpu_custom_call" | custom-call | flops 9395240960 | bytes 18743296 | tf_op jit(solution)/shard_map/g_up/pallas_call | solution.py:272
  378.3 0.0 copy-start.1
  378.3 0.0 copy-start.2
  378.3 51.7 %to_input.3 = (bf16[2048,896]{1,0:T(8,128)(2,1)}, bf16[56,2560]{1,0:T(8,128)(2,1)}, bf16[56,2560]{1,0:T(8,128)(2,1)}) custom-call(bf16[2048,2560]{1,0:T(8,128)(2,1)} %get-tuple-element.45.right.refs_0_, bf16[2048,2560]{1,0:T(8,128)(2,1)} %get-tuple-element.46.right.refs_1_, bf16[896,2560]{1,0:T(8,128)(2,1)} %bitcast.38, bf16[896,2560]{1,0:T(8,128)(2,1)} %bitcast.40, ...), custom_call_target="tpu_custom_call" | custom-call | flops 18790481920 | bytes 41156608 | tf_op jit(solution)/shard_map/to_input/pallas_call | solution.py:272
  430.0 0.0 copy-done.1
  430.0 0.0 copy-done.2
  430.0 0.9 pad_maximum_fusion.2
  430.9 0.0 reduce-scatter.3.cloned.1.call-done
  430.9 1.9 pad_maximum_fusion
  432.8 0.0 reduce-scatter.5.cloned.1.call-done
  432.8 1.9 pad_maximum_fusion.1
  434.7 4.2 copy.10
  (1 shorter events, 0.0 us)
Async XLA Ops:
  7.2 144.6 %all-gather.2.cloned.1.call-start = ((), (), s32[]{:S(2)}) async-start(), calls=%async_computation.2 | async-start | bytes 4874240 | tf_op jit(solution)/shard_map/all_gather | solution.py:357
  50.5 380.4 %reduce-scatter.3.cloned.1.call-start = ((), (), s32[]{:S(2)}) async-start(), calls=%async_computation.3 | async-start | bytes 4874240 | tf_op jit(solution)/shard_map/reduce_scatter | solution.py:403
  50.5 3.1 copy-start
  208.0 224.8 %reduce-scatter.5.cloned.1.call-start = ((), (), s32[]{:S(2)}) async-start(), calls=%async_computation.4 | async-start | bytes 4874240 | tf_op jit(solution)/shard_map/reduce_scatter | solution.py:403
  378.3 51.7 %copy-start.1 = (bf16[160,896]{1,0:T(8,128)(2,1)S(1)}, bf16[160,896]{1,0:T(8,128)(2,1)}, u32[]{:S(2)}) copy-start(bf16[160,896]{1,0:T(8,128)(2,1)} %get-tuple-element.51) | copy-start | bytes 860164
  378.3 51.7 %copy-start.2 = (bf16[160,896]{1,0:T(8,128)(2,1)S(1)}, bf16[160,896]{1,0:T(8,128)(2,1)}, u32[]{:S(2)}) copy-start(bf16[160,896]{1,0:T(8,128)(2,1)} %get-tuple-element.50) | copy-start | bytes 860164
Sparse Core Ops, SparseCore 0:
  50.6 50.2 all-gather.1
  208.1 67.9 reduce-scatter.2
  278.4 71.7 reduce-scatter.4
